TPU v7x, 32 devices: a whole 2x2x4 slice. The times are simulated.
32 devices in a mesh: replica: 4 (over z), shard: 8 (over y, x, core).
Axes of the slice: x: 2, y: 2, z: 4, core: 2. Of those that a mesh axis runs over, the one named last changes fastest.
Arguments:
- observations: bfloat16 [2048, 16, 1024], P(('replica', 'shard')), may hold values from -6 to 6
- rewards: float32 [2048, 16], P(('replica', 'shard')), may hold values from -6 to 6
- actions: int32 [2048, 21], P(('replica', 'shard')), may hold values from 0 to 17
- lengths: int32 [2048], P(('replica', 'shard')), may hold values from 1 to 16
- nsteps: int32 [2048], P(('replica', 'shard')), may hold values from 1 to 10
- prio_index: int32 [2048, 4], P(('replica', 'shard')), may hold values from 0 to 15
- assignment: int32 [2048, 1], P(('replica', 'shard')), may hold values from 0 to 3; in each aligned block of 64 rows (0 to 63, 64 to 127, ...) at most 32 rows name the same one
- rep_weight: bfloat16 [4, 1024, 512], P('replica', 'shard'), may hold values from -0.1875 to 0.1875
- dyn_in: bfloat16 [4, 512, 512], P('replica', 'shard'), may hold values from -0.25 to 0.25
- dyn_out: bfloat16 [4, 512, 512], P('replica', 'shard'), may hold values from -0.25 to 0.25
- value_hidden: bfloat16 [4, 512, 512], P('replica', 'shard'), may hold values from -0.25 to 0.25
- action_table: bfloat16 [4, 18, 512], P('replica'), may hold values from -6 to 6
- value_out: bfloat16 [4, 512], P('replica'), may hold values from -0.25 to 0.25
- reward_out: bfloat16 [4, 512], P('replica'), may hold values from -0.25 to 0.25
Outputs:
- priorities: float32 [2048, 4], P(('replica', 'shard'))
Inputs may be any that keep to these rules, and one draw needn't show every extreme that they name: `assignment`: among the 64 trajectories of one device (aligned blocks), at most 32 name one group; in some block one group is named by exactly 32.
All inputs are finite; a program needn't handle non-finite values.
Results may differ from a plain program's by a relative error of at most 0.0065.
Values may be sent and summed in bfloat16 or wider, within the bound.
A program may use at most 128 MiB of HBM per device.

v0:
```python
import math

import jax
import jax.numpy as jnp
from jax import lax
from jax.sharding import PartitionSpec as P

UNROLL = 5
PRIO = 4
MOSTG = 32


discount = 0.997
epsilon = 1e-06


def rms_scale(values):
    return values * lax.rsqrt(jnp.mean(values * values, axis=-1, keepdims=True) + epsilon)


def value_head(latent, hidden_weight, value_vector):
    inner = jnp.maximum(
        jnp.dot(latent, hidden_weight, preferred_element_type=jnp.float32), 0.0
    ).astype(jnp.bfloat16)
    return jnp.dot(inner, value_vector, preferred_element_type=jnp.float32)


def evaluate(frames, rewards, moves, lengths, nsteps, picks, network):
    rep_weight, dyn_in, dyn_out, value_hidden, action_table, value_out, reward_out = network
    batch, steps, width = frames.shape
    unroll = moves.shape[1] - steps
    flat = frames.reshape(batch * steps, width)
    latent = rms_scale(jnp.dot(flat, rep_weight, preferred_element_type=jnp.float32)).astype(
        jnp.bfloat16
    )
    root_value = value_head(latent, value_hidden, value_out).reshape(batch, steps)
    action_count = action_table.shape[0]
    model_return = jnp.zeros((batch * steps,), jnp.float32)
    state = latent
    for depth in range(unroll):
        chosen = moves[:, depth : depth + steps].reshape(batch * steps)
        one_hot = (chosen[:, None] == jnp.arange(action_count, dtype=jnp.int32)[None, :]).astype(
            jnp.bfloat16
        )
        embedded = jnp.dot(one_hot, action_table, preferred_element_type=jnp.float32)
        inner = jnp.maximum(
            jnp.dot(state, dyn_in, preferred_element_type=jnp.float32) + embedded, 0.0
        ).astype(jnp.bfloat16)
        update = jnp.dot(inner, dyn_out, preferred_element_type=jnp.float32)
        state = rms_scale(state.astype(jnp.float32) + update).astype(jnp.bfloat16)
        reward_guess = jnp.dot(state, reward_out, preferred_element_type=jnp.float32)
        model_return = model_return + discount**depth * reward_guess
    model_return = model_return + discount**unroll * value_head(state, value_hidden, value_out)
    model_return = model_return.reshape(batch, steps)
    position = jnp.arange(steps, dtype=jnp.int32)
    offset = position[None, :] - position[:, None]
    live = position[None, :] < lengths[:, None]
    horizon = nsteps[:, None, None]
    inside = (offset[None] >= 0) & (offset[None] < horizon) & live[:, None, :]
    power = discount ** jnp.maximum(offset, 0).astype(jnp.float32)
    weights = jnp.where(inside, power[None], 0.0)
    boot = (offset[None] == horizon) & live[:, None, :]
    boot_weights = jnp.where(boot, discount ** horizon.astype(jnp.float32), 0.0)
    target = jnp.sum(
        weights * rewards[:, None, :] + boot_weights * model_return[:, None, :], axis=2
    )
    priority = jnp.abs(target - root_value)
    pick = picks[:, :, None] == position[None, None, :]
    return jnp.sum(jnp.where(pick, priority[:, None, :], 0.0), axis=2)


def ranks_within(owner, groups):
    member = (owner[:, None] == jnp.arange(groups, dtype=jnp.int32)[None, :]).astype(jnp.int32)
    earlier = jnp.cumsum(member, axis=0) - member
    return jnp.sum(earlier * member, axis=1)


def pack_slots(spot, slots, frames, rewards, integers):
    match = spot[None, :] == jnp.arange(slots, dtype=jnp.int32)[:, None]
    source = jnp.sum(
        jnp.where(match, jnp.arange(spot.shape[0], dtype=jnp.int32)[None, :], 0), axis=1
    )
    return (
        jnp.take(frames, source, axis=0),
        jnp.take(rewards, source, axis=0),
        jnp.take(integers, source, axis=0),
    )


def evaluate_packed(received, network):
    frames, rewards, integers = received
    steps = frames.shape[-2]
    lead = tuple(frames.shape[:-2])
    count = math.prod(lead)
    flat_ints = integers.reshape(count, integers.shape[-1])
    result = evaluate(
        frames.reshape(count, steps, frames.shape[-1]),
        rewards.reshape(count, steps),
        flat_ints[:, : steps + UNROLL],
        flat_ints[:, steps + UNROLL],
        flat_ints[:, steps + UNROLL + 1],
        flat_ints[:, steps + UNROLL + 2 :],
        network,
    )
    return result.reshape(lead + (result.shape[-1],))


def on_device(
    observations,
    rewards,
    actions,
    lengths,
    nsteps,
    prio_index,
    assignment,
    rep_weight,
    dyn_in,
    dyn_out,
    value_hidden,
    action_table,
    value_out,
    reward_out,
):
    groups = lax.axis_size("replica")
    shards = lax.axis_size("shard")
    steps = observations.shape[1]
    width = observations.shape[2]
    capacity = -(-MOSTG // shards)
    owner = assignment[:, 0]
    rank = ranks_within(owner, groups)
    integers = jnp.concatenate([actions, lengths[:, None], nsteps[:, None], prio_index], axis=1)
    full_rep, full_in, full_out, full_value = (
        lax.all_gather(rep_weight, "shard", axis=1, tiled=True),
        lax.all_gather(dyn_in, "shard", axis=1, tiled=True),
        lax.all_gather(dyn_out, "shard", axis=1, tiled=True),
        lax.all_gather(value_hidden, "shard", axis=1, tiled=True),
    )
    spot = owner * (shards * capacity) + rank % shards * capacity + rank // shards
    slots = groups * shards * capacity
    frames, reward_rows, integer_rows = pack_slots(spot, slots, observations, rewards, integers)
    network = (
        full_rep[0],
        full_in[0],
        full_out[0],
        full_value[0],
        action_table[0],
        value_out[0],
        reward_out[0],
    )
    shaped = (
        frames.reshape(groups * shards, capacity, steps, width),
        reward_rows.reshape(groups * shards, capacity, steps),
        integer_rows.reshape(groups * shards, capacity, integer_rows.shape[-1]),
    )
    answered = evaluate_packed(
        (
            lax.all_to_all(
                shaped[0], ("replica", "shard"), split_axis=0, concat_axis=0, tiled=True
            ),
            lax.all_to_all(
                shaped[1].astype(jnp.bfloat16),
                ("replica", "shard"),
                split_axis=0,
                concat_axis=0,
                tiled=True,
            ).astype(jnp.float32),
            lax.all_to_all(
                shaped[2], ("replica", "shard"), split_axis=0, concat_axis=0, tiled=True
            ),
        ),
        network,
    )
    returned = lax.all_to_all(
        answered, ("replica", "shard"), split_axis=0, concat_axis=0, tiled=True
    )
    flat = returned.reshape(slots, PRIO)
    return jnp.take(flat, spot, axis=0)


def solution(mesh):
    placed = (
        P(("replica", "shard"), None, None),
        P(("replica", "shard"), None),
        P(("replica", "shard"), None),
        P(("replica", "shard")),
        P(("replica", "shard")),
        P(("replica", "shard"), None),
        P(("replica", "shard"), None),
        P("replica", "shard", None),
        P("replica", "shard", None),
        P("replica", "shard", None),
        P("replica", "shard", None),
        P("replica", None, None),
        P("replica", None),
        P("replica", None),
    )
    return jax.shard_map(
        on_device,
        mesh=mesh,
        in_specs=placed,
        out_specs=P(("replica", "shard"), None),
        check_vma=False,
    )
```

profile of v0, /device:TPU:0, one launch (start us, length us, event | category | flops | bytes accessed | tf_op | source)
XLA Modules:
  0.0 230.8 jit_solution(13169500135694591822)
XLA Ops:
  6.5 0.9 fusion.32
  7.5 0.8 select_reduce_fusion.2
  8.3 0.7 fusion.62
  9.2 0.8 copy.60
  10.0 0.7 gather_fusion.1
  10.8 0.7 select_convert_fusion
  11.5 7.3 %all-to-all-start.1 = ((bf16[32,4,16]{2,1,0:T(4,128)(2,1)}), bf16[32,4,16]{2,1,0:T(4,128)(2,1)S(1)}, u32[]{:S(2)}, u32[]{:S(2)}) async-start(bf16[32,4,16]{2,1,0:T(4,128)(2,1)} %select_convert_fusion), calls=%async_computation.1 | async-start | bytes 65536 | tf_op jit(solution)/shard_map/all_to_all | solution.py:160
  18.8 0.8 copy.55
  19.6 0.7 copy.56
  20.3 0.7 copy.57
  21.1 0.8 copy.58
  21.9 0.6 gather_fusion
  22.6 0.7 broadcast_select_fusion.1
  23.3 2.8 %gather_fusion.2 = bf16[128,16,1024]{2,1,0:T(8,128)(2,1)} fusion(bf16[64,16,1024]{2,1,0:T(8,128)(2,1)S(1)} %copy-done, s32[1024]{0:T(1024)S(1)} %pad_clamp_fusion.1), kind=kCustom, calls=%fused_computation.2 | custom fusion | bytes 8389120 | tf_op jit(solution)/shard_map/jit(_take)/gather | solution.py:84
  26.1 5.8 %all-to-all-start = ((s32[32,4,27]{2,1,0:T(4,128)}), s32[32,4,27]{2,1,0:T(4,128)S(1)}, u32[]{:S(2)}, u32[]{:S(2)}) async-start(s32[32,4,27]{2,1,0:T(4,128)} %broadcast_select_fusion.1), calls=%async_computation | async-start | bytes 131072 | tf_op jit(solution)/shard_map/all_to_all | solution.py:167
  32.0 4.6 %broadcast_select_fusion = bf16[32,4,16,1024]{3,2,1,0:T(8,128)(2,1)} fusion(bf16[32,4,16,1024]{3,2,1,0:T(8,128)(2,1)} %bitcast.146, pred[32,4]{1,0:T(8,128)(4,1)S(1)} %compare_and_fusion), kind=kLoop, calls=%fused_computation.28 | loop fusion | flops 2097152 | bytes 8388736 | tf_op jit(solution)/shard_map/jit(_take)/select_n | solution.py:84
  36.5 2.8 %all-to-all-done = s32[32,4,27]{2,1,0:T(4,128)S(1)} async-done(((s32[32,4,27]{2,1,0:T(4,128)}), s32[32,4,27]{2,1,0:T(4,128)S(1)}, u32[]{:S(2)}, u32[]{:S(2)}) %all-to-all-start) | async-done | bytes 13856 | tf_op jit(solution)/shard_map/all_to_all | solution.py:167
  39.4 3.6 %all-to-all-start.2 = ((bf16[32,4,16,1024]{3,2,1,0:T(8,128)(2,1)}), bf16[32,4,16,1024]{3,2,1,0:T(8,128)(2,1)}, u32[]{:S(2)}, u32[]{:S(2)}) async-start(bf16[32,4,16,1024]{3,2,1,0:T(8,128)(2,1)} %broadcast_select_fusion), calls=%async_computation.2 | async-start | bytes 8388608 | tf_op jit(solution)/shard_map/all_to_all | solution.py:157
  43.0 0.7 all-gather.2.cloned.1.call-update
  43.7 36.1 %all_gather.13 = bf16[1,512,512]{2,1,0:T(8,128)(2,1)S(1)} all-gather(bf16[1,64,512]{2,1,0:T(8,128)(2,1)S(1)} %copy-done.7), channel_id=1, replica_groups=mesh['replica'=4,'shard'=8] {'shard'}, dimensions={1}, use_global_device_ids=true | all-gather | bytes 589824 | tf_op jit(solution)/shard_map/all_gather | solution.py:134
  79.9 19.0 %all_gather.14 = bf16[1,512,512]{2,1,0:T(8,128)(2,1)S(1)} all-gather(bf16[1,64,512]{2,1,0:T(8,128)(2,1)S(1)} %copy-done.8), channel_id=1, replica_groups=mesh['replica'=4,'shard'=8] {'shard'}, dimensions={1}, use_global_device_ids=true | all-gather | bytes 589824 | tf_op jit(solution)/shard_map/all_gather | solution.py:135
  98.9 10.6 %all_gather.15 = bf16[1,512,512]{2,1,0:T(8,128)(2,1)} all-gather(bf16[1,64,512]{2,1,0:T(8,128)(2,1)S(1)} %copy-done.9), channel_id=1, replica_groups=mesh['replica'=4,'shard'=8] {'shard'}, dimensions={1}, use_global_device_ids=true | all-gather | bytes 589824 | tf_op jit(solution)/shard_map/all_gather | solution.py:136
  110.6 26.6 %all-to-all-done.2 = bf16[32,4,16,1024]{3,2,1,0:T(8,128)(2,1)} async-done(((bf16[32,4,16,1024]{3,2,1,0:T(8,128)(2,1)}), bf16[32,4,16,1024]{3,2,1,0:T(8,128)(2,1)}, u32[]{:S(2)}, u32[]{:S(2)}) %all-to-all-start.2) | async-done | bytes 4194336 | tf_op jit(solution)/shard_map/all_to_all | solution.py:157
  137.2 5.0 %multiply_reduce_fusion.5 = (f32[2048]{0:T(1024)S(1)}, f32[2048,512]{0,1:T(8,128)S(1)}) fusion(bf16[2048,1024]{1,0:T(8,128)(2,1)} %bitcast.12, bf16[1,1024,512]{2,1,0:T(8,128)(2,1)} %all-gather.2.cloned.1.call-done), kind=kOutput, calls=%fused_computation.27 | convolution fusion | flops 2149578752 | bytes 9445376 | tf_op jit(solution)/shard_map/dot_general | solution.py:33
  142.3 0.5 multiply_convert_fusion.5
  142.8 3.2 %fusion.20 = f32[2048,512]{1,0:T(8,128)} fusion(bf16[2048,512]{0,1:T(8,128)(2,1)S(1)} %multiply_convert_fusion.5, bf16[1,512,512]{2,1,0:T(8,128)(2,1)S(1)} %all_gather.13), kind=kOutput, calls=%fused_computation.53 | convolution fusion | flops 1073741824 | bytes 6815744 | tf_op jit(solution)/shard_map/dot_general | solution.py:47
  146.0 5.2 %multiply_reduce_fusion.4 = (f32[2048]{0:T(1024)S(1)}, f32[2048,512]{0,1:T(8,128)}) fusion(bf16[1,512,512]{2,1,0:T(8,128)(2,1)S(1)} %all_gather.14, f32[2048,512]{1,0:T(8,128)} %fusion.20, s32[2048]{0:T(1024)S(1)} %eq.138, bf16[1,18,512]{2,1,0:T(8,128)(2,1)S(1)} %copy-done.4, bf16[2048,512]{0,1:T(8,128)(2,1)S(1)} %multiply_convert_fusion.5), kind=kOutput, calls=%fused_computation.23 | convolution fusion | flops 1118865408 | bytes 11044864 | tf_op jit(solution)/shard_map/dot_general | solution.py:49
  151.2 2.7 %multiply_convert_fusion.4 = bf16[2048,512]{0,1:T(8,128)(2,1)S(1)} fusion(f32[2048,512]{0,1:T(8,128)} %get-tuple-element.17, f32[2048]{0:T(1024)S(1)} %add_rsqrt_fusion.4), kind=kLoop, calls=%fused_computation.22 | loop fusion | flops 2097152 | bytes 6299648 | tf_op jit(solution)/shard_map/convert_element_type | solution.py:50
  153.9 3.2 %fusion.18 = f32[2048,512]{1,0:T(8,128)} fusion(bf16[2048,512]{0,1:T(8,128)(2,1)S(1)} %multiply_convert_fusion.4, bf16[1,512,512]{2,1,0:T(8,128)(2,1)S(1)} %all_gather.13), kind=kOutput, calls=%fused_computation.51 | convolution fusion | flops 1073741824 | bytes 6815744 | tf_op jit(solution)/shard_map/dot_general | solution.py:47
  157.5 5.0 %multiply_reduce_fusion.3 = (f32[2048]{0:T(1024)S(1)}, f32[2048,512]{0,1:T(8,128)}) fusion(bf16[1,512,512]{2,1,0:T(8,128)(2,1)S(1)} %all_gather.14, f32[2048,512]{1,0:T(8,128)} %fusion.18, s32[2048]{0:T(1024)S(1)} %eq.142, bf16[1,18,512]{2,1,0:T(8,128)(2,1)S(1)} %copy-done.4, bf16[2048,512]{0,1:T(8,128)(2,1)S(1)} %multiply_convert_fusion.4), kind=kOutput, calls=%fused_computation.19 | convolution fusion | flops 1118865408 | bytes 11044864 | tf_op jit(solution)/shard_map/dot_general | solution.py:49
  162.6 2.7 %multiply_convert_fusion.3 = bf16[2048,512]{0,1:T(8,128)(2,1)S(1)} fusion(f32[2048,512]{0,1:T(8,128)} %get-tuple-element.19, f32[2048]{0:T(1024)S(1)} %add_rsqrt_fusion.3), kind=kLoop, calls=%fused_computation.18 | loop fusion | flops 2097152 | bytes 6299648 | tf_op jit(solution)/shard_map/convert_element_type | solution.py:50
  165.7 3.2 %fusion.16 = f32[2048,512]{1,0:T(8,128)} fusion(bf16[2048,512]{0,1:T(8,128)(2,1)S(1)} %multiply_convert_fusion.3, bf16[1,512,512]{2,1,0:T(8,128)(2,1)S(1)} %all_gather.13), kind=kOutput, calls=%fused_computation.49 | convolution fusion | flops 1073741824 | bytes 6815744 | tf_op jit(solution)/shard_map/dot_general | solution.py:47
  168.9 5.0 %multiply_reduce_fusion.2 = (f32[2048]{0:T(1024)S(1)}, f32[2048,512]{0,1:T(8,128)}) fusion(bf16[1,512,512]{2,1,0:T(8,128)(2,1)S(1)} %all_gather.14, f32[2048,512]{1,0:T(8,128)} %fusion.16, s32[2048]{0:T(1024)S(1)} %eq.146, bf16[1,18,512]{2,1,0:T(8,128)(2,1)S(1)} %copy-done.4, bf16[2048,512]{0,1:T(8,128)(2,1)S(1)} %multiply_convert_fusion.3), kind=kOutput, calls=%fused_computation.15 | convolution fusion | flops 1118865408 | bytes 11044864 | tf_op jit(solution)/shard_map/dot_general | solution.py:49
  173.9 2.7 %multiply_convert_fusion.2 = bf16[2048,512]{0,1:T(8,128)(2,1)S(1)} fusion(f32[2048,512]{0,1:T(8,128)} %get-tuple-element.21, f32[2048]{0:T(1024)S(1)} %add_rsqrt_fusion.2), kind=kLoop, calls=%fused_computation.14 | loop fusion | flops 2097152 | bytes 6299648 | tf_op jit(solution)/shard_map/convert_element_type | solution.py:50
  177.0 3.2 %fusion.14 = f32[2048,512]{1,0:T(8,128)} fusion(bf16[2048,512]{0,1:T(8,128)(2,1)S(1)} %multiply_convert_fusion.2, bf16[1,512,512]{2,1,0:T(8,128)(2,1)S(1)} %all_gather.13), kind=kOutput, calls=%fused_computation.47 | convolution fusion | flops 1073741824 | bytes 6815744 | tf_op jit(solution)/shard_map/dot_general | solution.py:47
  180.2 5.0 %multiply_reduce_fusion.1 = (f32[2048]{0:T(1024)S(1)}, f32[2048,512]{0,1:T(8,128)}) fusion(bf16[1,512,512]{2,1,0:T(8,128)(2,1)S(1)} %all_gather.14, f32[2048,512]{1,0:T(8,128)} %fusion.14, s32[2048]{0:T(1024)S(1)} %eq.150, bf16[1,18,512]{2,1,0:T(8,128)(2,1)S(1)} %copy-done.4, bf16[2048,512]{0,1:T(8,128)(2,1)S(1)} %multiply_convert_fusion.2), kind=kOutput, calls=%fused_computation.11 | convolution fusion | flops 1118865408 | bytes 11044864 | tf_op jit(solution)/shard_map/dot_general | solution.py:49
  185.3 2.7 %multiply_convert_fusion.1 = bf16[2048,512]{0,1:T(8,128)(2,1)S(1)} fusion(f32[2048,512]{0,1:T(8,128)} %get-tuple-element.23, f32[2048]{0:T(1024)S(1)} %add_rsqrt_fusion.1), kind=kLoop, calls=%fused_computation.10 | loop fusion | flops 2097152 | bytes 6299648 | tf_op jit(solution)/shard_map/convert_element_type | solution.py:50
  188.3 3.2 %fusion.12 = f32[2048,512]{1,0:T(8,128)} fusion(bf16[2048,512]{0,1:T(8,128)(2,1)S(1)} %multiply_convert_fusion.1, bf16[1,512,512]{2,1,0:T(8,128)(2,1)S(1)} %all_gather.13), kind=kOutput, calls=%fused_computation.45 | convolution fusion | flops 1073741824 | bytes 6815744 | tf_op jit(solution)/shard_map/dot_general | solution.py:47
  191.6 2.7 %maximum_convert_fusion = bf16[2048,512]{1,0:T(8,128)(2,1)} fusion(bf16[2048,512]{0,1:T(8,128)(2,1)S(1)} %copy-done.3, bf16[1,512,512]{2,1,0:T(8,128)(2,1)S(1)} %copy-done.5), kind=kOutput, calls=%fused_computation.4 | convolution fusion | flops 1075838976 | bytes 4718592 | tf_op jit(solution)/shard_map/dot_general | solution.py:23
  194.3 5.0 %multiply_reduce_fusion = (f32[2048]{0:T(1024)S(1)}, f32[2048,512]{0,1:T(8,128)}) fusion(bf16[1,512,512]{2,1,0:T(8,128)(2,1)S(1)} %all_gather.14, f32[2048,512]{1,0:T(8,128)} %fusion.12, s32[2048]{0:T(1024)S(1)} %eq.154, bf16[1,18,512]{2,1,0:T(8,128)(2,1)S(1)} %copy-done.4, bf16[2048,512]{0,1:T(8,128)(2,1)S(1)} %multiply_convert_fusion.1), kind=kOutput, calls=%fused_computation.7 | convolution fusion | flops 1118865408 | bytes 11044864 | tf_op jit(solution)/shard_map/dot_general | solution.py:49
  199.3 2.7 %fusion.3 = f32[1,2048]{1,0:T(1,128)S(1)} fusion(f32[2048,512]{0,1:T(8,128)} %get-tuple-element.25, f32[2048]{0:T(1024)S(1)} %add_rsqrt_fusion, bf16[1,512]{1,0:T(2,128)(2,1)S(1)} %copy-done.10), kind=kOutput, calls=%fused_computation.37 | convolution fusion | flops 4194304 | bytes 4211712 | tf_op jit(solution)/shard_map/dot_general | solution.py:51
  202.1 3.9 %fusion = f32[1,2048]{1,0:T(1,128)S(1)} fusion(f32[2048,512]{0,1:T(8,128)} %get-tuple-element.25, f32[2048]{0:T(1024)S(1)} %add_rsqrt_fusion, bf16[1,512,512]{2,1,0:T(8,128)(2,1)S(1)} %copy-done.6, bf16[1,512]{1,0:T(2,128)(2,1)S(1)} %copy-done.12), kind=kOutput, calls=%fused_computation.29 | convolution fusion | flops 1080033280 | bytes 4736000 | tf_op jit(solution)/shard_map/dot_general | solution.py:25
  206.0 4.1 %fusion.45 = f32[1,128,16]{2,0,1:T(1,128)S(1)} fusion(bf16[128,16,512]{2,1,0:T(8,128)(2,1)} %bitcast.150, bf16[1,512]{1,0:T(2,128)(2,1)S(1)} %copy-done.12), kind=kOutput, calls=%fused_computation.98 | convolution fusion | flops 2097152 | bytes 2106368 | tf_op jit(solution)/shard_map/dot_general | solution.py:25
  210.7 0.7 copy.63
  211.4 3.5 %all-to-all-start.3 = ((f32[32,4,4]{1,2,0:T(4,128)}), f32[32,4,4]{1,2,0:T(4,128)S(1)}, u32[]{:S(2)}, u32[]{:S(2)}) async-start(f32[32,4,4]{1,2,0:T(4,128)} %copy.63), calls=%async_computation.3 | async-start | bytes 131072 | tf_op jit(solution)/shard_map/all_to_all | solution.py:173
  215.0 7.4 %all-to-all-done.3 = f32[32,4,4]{1,2,0:T(4,128)S(1)} async-done(((f32[32,4,4]{1,2,0:T(4,128)}), f32[32,4,4]{1,2,0:T(4,128)S(1)}, u32[]{:S(2)}, u32[]{:S(2)}) %all-to-all-start.3) | async-done | bytes 2080 | tf_op jit(solution)/shard_map/all_to_all | solution.py:173
  222.7 0.6 gather_fusion.3
  223.3 0.7 copy.65
  (73 shorter events, 4.1 us)
Async XLA Ops:
  6.5 16.8 %copy-start = (bf16[64,16,1024]{2,1,0:T(8,128)(2,1)S(1)}, bf16[64,16,1024]{2,1,0:T(8,128)(2,1)}, u32[]{:S(2)}) copy-start(bf16[64,16,1024]{2,1,0:T(8,128)(2,1)} %param.14) | copy-start | bytes 6291460
  11.5 14.7 %all-to-all-start.1 = ((bf16[32,4,16]{2,1,0:T(4,128)(2,1)}), bf16[32,4,16]{2,1,0:T(4,128)(2,1)S(1)}, u32[]{:S(2)}, u32[]{:S(2)}) async-start(bf16[32,4,16]{2,1,0:T(4,128)(2,1)} %select_convert_fusion), calls=%async_computation.1 | async-start | bytes 65536 | tf_op jit(solution)/shard_map/all_to_all | solution.py:160
  26.1 13.3 %all-to-all-start = ((s32[32,4,27]{2,1,0:T(4,128)}), s32[32,4,27]{2,1,0:T(4,128)S(1)}, u32[]{:S(2)}, u32[]{:S(2)}) async-start(s32[32,4,27]{2,1,0:T(4,128)} %broadcast_select_fusion.1), calls=%async_computation | async-start | bytes 131072 | tf_op jit(solution)/shard_map/all_to_all | solution.py:167
  36.5 7.2 %copy-start.7 = (bf16[1,64,512]{2,1,0:T(8,128)(2,1)S(1)}, bf16[1,64,512]{2,1,0:T(8,128)(2,1)}, u32[]{:S(2)}) copy-start(bf16[1,64,512]{2,1,0:T(8,128)(2,1)} %param.22) | copy-start | bytes 196612
  36.5 43.4 %copy-start.8 = (bf16[1,64,512]{2,1,0:T(8,128)(2,1)S(1)}, bf16[1,64,512]{2,1,0:T(8,128)(2,1)}, u32[]{:S(2)}) copy-start(bf16[1,64,512]{2,1,0:T(8,128)(2,1)} %param.23) | copy-start | bytes 196612
  36.5 62.4 %copy-start.9 = (bf16[1,64,512]{2,1,0:T(8,128)(2,1)S(1)}, bf16[1,64,512]{2,1,0:T(8,128)(2,1)}, u32[]{:S(2)}) copy-start(bf16[1,64,512]{2,1,0:T(8,128)(2,1)} %param.24) | copy-start | bytes 196612
  36.5 73.0 %copy-start.11 = (s32[64,1]{0,1:T(1,128)S(1)}, s32[64,1]{0,1:T(1,128)}, u32[]{:S(2)}) copy-start(s32[64,1]{0,1:T(1,128)} %param.20) | copy-start | bytes 772
  39.4 97.8 %all-to-all-start.2 = ((bf16[32,4,16,1024]{3,2,1,0:T(8,128)(2,1)}), bf16[32,4,16,1024]{3,2,1,0:T(8,128)(2,1)}, u32[]{:S(2)}, u32[]{:S(2)}) async-start(bf16[32,4,16,1024]{3,2,1,0:T(8,128)(2,1)} %broadcast_select_fusion), calls=%async_computation.2 | async-start | bytes 8388608 | tf_op jit(solution)/shard_map/all_to_all | solution.py:157
  42.9 67.6 %all-gather.2.cloned.1.call-start = ((), (), s32[]{:S(2)}) async-start(), calls=%async_computation.4 | async-start | bytes 1179648 | tf_op jit(solution)/shard_map/all_gather | solution.py:133
  142.8 3.2 %copy-start.2 = (bf16[2048,512]{0,1:T(8,128)(2,1)}, bf16[2048,512]{0,1:T(8,128)(2,1)S(1)}, u32[]{:S(2)}) copy-start(bf16[2048,512]{0,1:T(8,128)(2,1)S(1)} %multiply_convert_fusion.5) | copy-start | bytes 6291460
  142.8 3.2 %copy-start.4 = (bf16[1,18,512]{2,1,0:T(8,128)(2,1)S(1)}, bf16[1,18,512]{2,1,0:T(8,128)(2,1)}, u32[]{:S(2)}) copy-start(bf16[1,18,512]{2,1,0:T(8,128)(2,1)} %param.25) | copy-start | bytes 55300
  153.9 3.2 %copy-start.10 = (bf16[1,512]{1,0:T(2,128)(2,1)S(1)}, bf16[1,512]{1,0:T(2,128)(2,1)}, u32[]{:S(2)}) copy-start(bf16[1,512]{1,0:T(2,128)(2,1)} %param.27) | copy-start | bytes 3076
  188.3 3.2 %copy-start.3 = (bf16[2048,512]{0,1:T(8,128)(2,1)S(1)}, bf16[2048,512]{0,1:T(8,128)(2,1)}, u32[]{:S(2)}) copy-start(bf16[2048,512]{0,1:T(8,128)(2,1)} %copy-done.2) | copy-start | bytes 6291460
  188.3 3.2 %copy-start.5 = (bf16[1,512,512]{2,1,0:T(8,128)(2,1)S(1)}, bf16[1,512,512]{2,1,0:T(8,128)(2,1)}, u32[]{:S(2)}) copy-start(bf16[1,512,512]{2,1,0:T(8,128)(2,1)} %all_gather.15) | copy-start | bytes 1572868
  199.3 2.8 %copy-start.6 = (bf16[1,512,512]{2,1,0:T(8,128)(2,1)S(1)}, bf16[1,512,512]{2,1,0:T(8,128)(2,1)}, u32[]{:S(2)}) copy-start(bf16[1,512,512]{2,1,0:T(8,128)(2,1)} %all_gather.15) | copy-start | bytes 1572868
  199.3 2.8 %copy-start.12 = (bf16[1,512]{1,0:T(2,128)(2,1)S(1)}, bf16[1,512]{1,0:T(2,128)(2,1)}, u32[]{:S(2)}) copy-start(bf16[1,512]{1,0:T(2,128)(2,1)} %param.26) | copy-start | bytes 3076
  199.3 24.7 %copy-start.1 = (bf16[64,16,1024]{2,1,0:T(8,128)(2,1)S(1)}, bf16[64,16,1024]{2,1,0:T(8,128)(2,1)}, u32[]{:S(2)}) copy-start(bf16[64,16,1024]{2,1,0:T(8,128)(2,1)} %param.14) | copy-start | bytes 6291460
  211.4 11.0 %all-to-all-start.3 = ((f32[32,4,4]{1,2,0:T(4,128)}), f32[32,4,4]{1,2,0:T(4,128)S(1)}, u32[]{:S(2)}, u32[]{:S(2)}) async-start(f32[32,4,4]{1,2,0:T(4,128)} %copy.63), calls=%async_computation.3 | async-start | bytes 131072 | tf_op jit(solution)/shard_map/all_to_all | solution.py:173
Sparse Core Ops, SparseCore 0:
  45.6 37.9 all-gather.1
where the time goes:
time: 232 us; the launch traced here: 231 us
  blocking collectives  65.8 us (28%)
  matrix products  61.6 us (27%)
  waiting for transfers between devices  37.6 us (16%)
  other arithmetic  20.3 us (9%)
  starting transfers between devices  20.3 us (9%)
  between operations  13.7 us (6%)
  local copies, waits for them, and re-layouts  11.7 us (5%)
    all_gather x1, blocking collectives, on_device(): lax.all_gather(dyn_in, 'shard', axis=1, tiled=True)  36.1 us
    all_to_all x1, waiting for transfers between devices, on_device(): lax.all_to_all(shaped[0], ('replica', 'shard'), split_axis=0, concat_axis...  26.6 us
    dot_general x5, matrix products, evaluate(): update = jnp.dot(inner, dyn_out, preferred_element_type=jnp.float32)  25.4 us
    all_gather x1, blocking collectives, on_device(): lax.all_gather(dyn_out, 'shard', axis=1, tiled=True)  19 us
    dot_general x5, matrix products, evaluate(): jnp.dot(state, dyn_in, preferred_element_type=jnp.float32) + embedded  16.1 us
    convert_element_type x4, other arithmetic, evaluate(): state = rms_scale(state.astype(jnp.float32) + update).astype(jnp.bfloat16)  10.7 us
    all_gather x1, blocking collectives, on_device(): lax.all_gather(value_hidden, 'shard', axis=1, tiled=True)  10.6 us
    dot_general x2, matrix products, value_head(): return jnp.dot(inner, value_vector, preferred_element_type=jnp.float32)  8.07 us
  transfers between devices with their start and end apart: 5, of which 3 were waited for; matrix products, arithmetic and copies ran while one was open for 6% of the time, Pallas kernels for 0%

commit v1 on v0

v1 whole, which is shorter than its diff:
```python
import jax
import jax.numpy as jnp
from jax import lax
from jax.sharding import PartitionSpec as P

MOSTG = 32


discount = 0.997
epsilon = 1e-06


def rms_scale(values):
    return values * lax.rsqrt(jnp.mean(values * values, axis=-1, keepdims=True) + epsilon)


def matmul(rows, weights):
    return jnp.einsum("gmk,gkn->gmn", rows, weights, preferred_element_type=jnp.float32)


def ranks_within(owner, groups):
    member = (owner[:, None] == jnp.arange(groups, dtype=jnp.int32)[None, :]).astype(jnp.int32)
    earlier = jnp.cumsum(member, axis=0) - member
    return jnp.sum(earlier * member, axis=1)


def reward_part(rewards, lengths, nsteps, picks):
    position = jnp.arange(rewards.shape[1], dtype=jnp.int32)
    offset = position[None, None, :] - picks[:, :, None]
    inside = (
        (offset >= 0)
        & (offset < nsteps[:, None, None])
        & (position[None, None, :] < lengths[:, None, None])
    )
    power = discount ** jnp.maximum(offset, 0).astype(jnp.float32)
    return jnp.sum(jnp.where(inside, power, 0.0) * rewards[:, None, :], axis=2)


def on_device(
    observations,
    rewards,
    actions,
    lengths,
    nsteps,
    prio_index,
    assignment,
    rep_weight,
    dyn_in,
    dyn_out,
    value_hidden,
    action_table,
    value_out,
    reward_out,
):
    groups = lax.axis_size("replica")
    batch, steps, width = observations.shape
    unroll = actions.shape[1] - steps
    picks = prio_index.shape[1]
    both = ("replica", "shard")

    def whole(weight):
        part = lax.all_gather(weight, both, axis=0, tiled=True)
        return part.reshape(groups, -1, weight.shape[-1])

    full_rep, full_in, full_out, full_value = (
        whole(rep_weight),
        whole(dyn_in),
        whole(dyn_out),
        whole(value_hidden),
    )
    small = jnp.concatenate([action_table[0], value_out, reward_out], axis=0)
    small = lax.all_gather(small, "replica", axis=0)
    action_count = action_table.shape[1]
    tables = small[:, :action_count]
    value_vector = small[:, action_count]
    reward_vector = small[:, action_count + 1]

    owner = assignment[:, 0]
    spot = owner * MOSTG + ranks_within(owner, groups)
    slots = groups * MOSTG
    match = spot[None, :] == jnp.arange(slots, dtype=jnp.int32)[:, None]
    source = jnp.sum(
        jnp.where(match, jnp.arange(batch, dtype=jnp.int32)[None, :], 0), axis=1
    )
    reach = prio_index + nsteps[:, None]
    alive = reach < lengths[:, None]
    reach = jnp.minimum(reach, steps - 1)
    base = jnp.arange(batch, dtype=jnp.int32)[:, None] * steps
    rows = jnp.concatenate([base + prio_index, base + reach], axis=1)
    moves = jnp.concatenate(
        [jnp.take_along_axis(actions, reach + depth, axis=1) for depth in range(unroll)], axis=1
    )
    packed = jnp.take(jnp.concatenate([rows, moves], axis=1), source, axis=0)
    packed = packed.reshape(groups, MOSTG, (2 + unroll), picks).transpose(0, 2, 1, 3)
    packed = packed.reshape(groups, 2 + unroll, MOSTG * picks)
    lines = packed[:, :2].reshape(-1)
    frames = jnp.take(observations.reshape(batch * steps, width), lines, axis=0)
    frames = frames.reshape(groups, 2 * MOSTG * picks, width)

    latent = rms_scale(matmul(frames, full_rep)).astype(jnp.bfloat16)
    state = latent[:, MOSTG * picks :]
    model_return = 0.0
    for depth in range(unroll):
        chosen = packed[:, 2 + depth]
        one_hot = (
            chosen[:, :, None] == jnp.arange(action_count, dtype=jnp.int32)[None, None, :]
        ).astype(jnp.bfloat16)
        inner = jnp.maximum(matmul(state, full_in) + matmul(one_hot, tables), 0.0).astype(
            jnp.bfloat16
        )
        state = rms_scale(state.astype(jnp.float32) + matmul(inner, full_out)).astype(
            jnp.bfloat16
        )
        guess = jnp.einsum(
            "gmk,gk->gm", state, reward_vector, preferred_element_type=jnp.float32
        )
        model_return = model_return + discount**depth * guess
    ends = jnp.concatenate([latent[:, : MOSTG * picks], state], axis=1)
    hidden = jnp.maximum(matmul(ends, full_value), 0.0).astype(jnp.bfloat16)
    values = jnp.einsum(
        "gmk,gk->gm", hidden, value_vector, preferred_element_type=jnp.float32
    )
    root_value = values[:, : MOSTG * picks].reshape(slots, picks)
    model_return = model_return + discount**unroll * values[:, MOSTG * picks :]
    model_return = model_return.reshape(slots, picks)
    back = jnp.take(jnp.concatenate([root_value, model_return], axis=1), spot, axis=0)
    bonus = discount ** nsteps.astype(jnp.float32)
    target = reward_part(rewards, lengths, nsteps, prio_index) + jnp.where(
        alive, bonus[:, None] * back[:, picks:], 0.0
    )
    return jnp.abs(target - back[:, :picks])


def solution(mesh):
    placed = (
        P(("replica", "shard"), None, None),
        P(("replica", "shard"), None),
        P(("replica", "shard"), None),
        P(("replica", "shard")),
        P(("replica", "shard")),
        P(("replica", "shard"), None),
        P(("replica", "shard"), None),
        P("replica", "shard", None),
        P("replica", "shard", None),
        P("replica", "shard", None),
        P("replica", "shard", None),
        P("replica", None, None),
        P("replica", None),
        P("replica", None),
    )
    return jax.shard_map(
        on_device,
        mesh=mesh,
        in_specs=placed,
        out_specs=P(("replica", "shard"), None),
        check_vma=False,
    )
```

time: 232 us -> 260 us (1.12)
  waiting for transfers between devices: 37.6 us -> 156 us
  blocking collectives: 65.8 us -> 15.2 us
  starting transfers between devices: 20.3 us -> 0.12 us
  matrix products: 61.6 us -> 41.7 us
  local copies, waits for them, and re-layouts: 11.7 us -> 22.7 us
  other arithmetic: 20.3 us -> 9.86 us
    all_gather x1 -> x4, waiting for transfers between devices: 0.02 us -> 153 us  [whole(): part = lax.all_gather(weight, both, axis=0, tiled=True)]
    all_gather x3 -> x1, blocking collectives: 65.8 us -> 15.2 us  [on_device(): small = lax.all_gather(small, 'replica', axis=0)]
    all_to_all x4 -> x0, waiting for transfers between devices: 36.8 us -> none  [the longest x1 26.6 us: on_device(): lax.all_to_all(shaped[0], ('replica', 'shard'), split_axis=0, concat_axis...]
    all_to_all x4 -> x0, starting transfers between devices: 20.3 us -> none  [the longest x1 7.32 us: on_device(): lax.all_to_all(shaped[1].astype(jnp.bfloat16), ('replica', 'shard'), spli...]
    dot_general x19 -> x17, matrix products: 61.6 us -> 41.7 us  [the longest x11 35.7 us: matmul(): jnp.einsum('gmk,gkn->gmn', rows, weights, preferred_element_type=jnp.floa...]
    gather x4 -> x31, local copies, waits for them, and re-layouts: 4.74 us -> 18.8 us  [the longest x25 12 us: on_device(): jnp.take_along_axis(actions, reach + depth, axis=1)]
    convert_element_type x6, other arithmetic: 11.9 us -> 5.81 us  [the longest x5 5.6 us: on_device(): rms_scale(state.astype(jnp.float32) + matmul(inner, full_out))]
    select_n x4, other arithmetic: 5.38 us -> 0.03 us  [the longest x1 0.01 us: on_device(): jnp.take_along_axis(actions, reach + depth, axis=1)]
  transfers between devices with their start and end apart: 5 -> 4, of which waited for: 3 -> 4; matrix products, arithmetic and copies ran while one was open for 6% -> 27% of each run, Pallas kernels for 0% -> 0%
where the time goes in v1:
time: 260 us; the launch traced here: 259 us
  waiting for transfers between devices  156 us (60%)
  matrix products  41.7 us (16%)
  local copies, waits for them, and re-layouts  22.7 us (9%)
  blocking collectives  15.2 us (6%)
  between operations  13.6 us (5%)
  other arithmetic  9.86 us (4%)
    all_gather x4, waiting for transfers between devices, whole(): part = lax.all_gather(weight, both, axis=0, tiled=True)  153 us
    dot_general x11, matrix products, matmul(): jnp.einsum('gmk,gkn->gmn', rows, weights, preferred_element_type=jnp.floa...  35.7 us
    all_gather x1, blocking collectives, on_device(): small = lax.all_gather(small, 'replica', axis=0)  15.2 us
    gather x25, local copies, waits for them, and re-layouts, on_device(): jnp.take_along_axis(actions, reach + depth, axis=1)  12 us
    convert_element_type x5, other arithmetic, on_device(): rms_scale(state.astype(jnp.float32) + matmul(inner, full_out))  5.6 us
    gather x1, local copies, waits for them, and re-layouts, on_device(): frames = jnp.take(observations.reshape(batch * steps, width), lines, axis=0)  5.35 us
  transfers between devices with their start and end apart: 4, of which 4 were waited for; matrix products, arithmetic and copies ran while one was open for 27% of the time, Pallas kernels for 0%

profile of v1, /device:TPU:0, one launch (start us, length us, event | category | flops | bytes accessed | tf_op | source)
XLA Modules:
  0.0 259.0 jit_solution(17733160215500680580)
XLA Ops:
  6.5 0.7 all-gather.7.cloned.1.call-update
  7.3 0.7 all-gather.9.cloned.1.call-update
  8.1 0.7 all-gather.11.cloned.1.call-update
  8.8 0.5 all-gather.13.cloned.1.call-update
  9.3 0.7 fusion.39
  10.2 0.8 select_reduce_fusion.1
  11.0 0.7 multiply_add_fusion
  11.9 0.7 bitcast_or_fusion
  12.8 2.0 gather_fusion.5
  15.2 2.0 gather_fusion.6
  17.6 2.0 gather_fusion.3
  20.0 2.0 gather_fusion.4
  22.5 2.0 gather_fusion.7
  24.9 0.6 gather_fusion
  25.8 0.2 copy.108
  26.1 0.3 reshape.199
  26.5 15.2 %all-gather.1 = bf16[4,20,512]{2,1,0:T(8,128)(2,1)S(1)} all-gather(bf16[1,20,512]{2,1,0:T(8,128)(2,1)S(1)} %maximum_bitcast_fusion), channel_id=2, replica_groups=mesh['replica'=4,'shard'=8] {'replica'}, dimensions={0}, use_global_device_ids=true | all-gather | bytes 102400 | tf_op jit(solution)/shard_map/all_gather | solution.py:72
  41.8 5.3 %gather_fusion.1 = bf16[1024,1024]{1,0:T(8,128)(2,1)} fusion(bf16[1024,1024]{1,0:T(8,128)(2,1)S(1)} %bitcast.111, s32[1024]{0:T(1024)S(1)} %broadcast_clamp_fusion), kind=kCustom, calls=%fused_computation.6 | custom fusion | bytes 4198400 | tf_op jit(solution)/shard_map/jit(_take)/gather | solution.py:97
  47.2 27.3 %all-gather.7.cloned.1.call-done = bf16[32,128,512]{2,1,0:T(8,128)(2,1)} async-done(((bf16[1,128,512]{2,1,0:T(8,128)(2,1)}), bf16[32,128,512]{2,1,0:T(8,128)(2,1)}) %all-gather.7.cloned.1.call-update) | async-done | bytes 4194320 | tf_op jit(solution)/shard_map/all_gather | solution.py:62
  74.5 4.2 %multiply_reduce_fusion = (f32[4,256]{1,0:T(4,128)S(1)}, f32[4,256,512]{2,1,0:T(8,128)S(1)}) fusion(bf16[4,1024,512]{2,1,0:T(8,128)(2,1)} %bitcast.135, bf16[4,256,1024]{2,1,0:T(8,128)(2,1)} %bitcast.122, pred[4,256]{1,0:T(4,128)(4,1)S(1)} %compare_and_fusion), kind=kOutput, calls=%fused_computation.10 | convolution fusion | flops 1075837952 | bytes 8393728 | tf_op jit(solution)/shard_map/gmk,gkn->gmn/dot_general | solution.py:18
  78.7 0.2 multiply_convert_fusion
  78.9 53.4 %all-gather.9.cloned.1.call-done = bf16[32,64,512]{2,1,0:T(8,128)(2,1)} async-done(((bf16[1,64,512]{2,1,0:T(8,128)(2,1)}), bf16[32,64,512]{2,1,0:T(8,128)(2,1)}) %all-gather.9.cloned.1.call-update) | async-done | bytes 2097168 | tf_op jit(solution)/shard_map/all_gather | solution.py:62
  132.4 3.1 %fusion.27 = f32[4,128,512]{2,1,0:T(8,128)} fusion(bf16[4,512,512]{2,1,0:T(8,128)(2,1)} %bitcast.112, bf16[4,256,512]{2,1,0:T(8,128)(2,1)S(1)} %multiply_convert_fusion), kind=kOutput, calls=%fused_computation.55 | convolution fusion | flops 268435456 | bytes 3670016 | tf_op jit(solution)/shard_map/gmk,gkn->gmn/dot_general | solution.py:18
  135.4 54.9 %all-gather.11.cloned.1.call-done = bf16[32,64,512]{2,1,0:T(8,128)(2,1)} async-done(((bf16[1,64,512]{2,1,0:T(8,128)(2,1)}), bf16[32,64,512]{2,1,0:T(8,128)(2,1)}) %all-gather.11.cloned.1.call-update) | async-done | bytes 2097168 | tf_op jit(solution)/shard_map/all_gather | solution.py:62
  190.3 3.5 %multiply_reduce_fusion.5 = (f32[4,128]{1,0:T(4,128)S(1)}, f32[4,128,512]{2,1,0:T(8,128)}) fusion(bf16[4,512,512]{2,1,0:T(8,128)(2,1)} %bitcast.117, f32[4,128,512]{2,1,0:T(8,128)} %fusion.27, bf16[4,20,512]{2,1,0:T(8,128)(2,1)S(1)} %all-gather.1, s32[4,128]{1,0:T(4,128)S(1)} %get-tuple-element.14, bf16[4,256,512]{2,1,0:T(8,128)(2,1)S(1)} %multiply_convert_fusion), kind=kOutput, calls=%fused_computation.48 | convolution fusion | flops 279716352 | bytes 4804608 | tf_op jit(solution)/shard_map/gmk,gkn->gmn/dot_general | solution.py:18
  193.8 1.4 multiply_convert_fusion.5
  195.2 3.1 %fusion.81 = f32[4,128,512]{2,1,0:T(8,128)} fusion(bf16[4,128,512]{2,1,0:T(8,128)(2,1)S(1)} %multiply_convert_fusion.5, bf16[4,512,512]{2,1,0:T(8,128)(2,1)} %bitcast.113), kind=kOutput, calls=%fused_computation.154 | convolution fusion | flops 268435456 | bytes 3670016 | tf_op jit(solution)/shard_map/gmk,gkn->gmn/dot_general | solution.py:18
  198.3 3.6 %multiply_reduce_fusion.4 = (f32[4,128]{1,0:T(4,128)S(1)}, f32[4,128,512]{2,1,0:T(8,128)}) fusion(bf16[4,512,512]{2,1,0:T(8,128)(2,1)} %bitcast.118, f32[4,128,512]{2,1,0:T(8,128)} %fusion.81, bf16[4,20,512]{2,1,0:T(8,128)(2,1)S(1)} %all-gather.1, s32[4,128]{1,0:T(4,128)S(1)} %get-tuple-element.13, bf16[4,128,512]{2,1,0:T(8,128)(2,1)S(1)} %multiply_convert_fusion.5), kind=kOutput, calls=%fused_computation.46 | convolution fusion | flops 279716352 | bytes 4804608 | tf_op jit(solution)/shard_map/gmk,gkn->gmn/dot_general | solution.py:18
  201.8 1.4 multiply_convert_fusion.4
  203.2 3.0 %fusion.82 = f32[4,128,512]{2,1,0:T(8,128)} fusion(bf16[4,128,512]{2,1,0:T(8,128)(2,1)S(1)} %multiply_convert_fusion.4, bf16[4,512,512]{2,1,0:T(8,128)(2,1)} %bitcast.114), kind=kOutput, calls=%fused_computation.155 | convolution fusion | flops 268435456 | bytes 3670016 | tf_op jit(solution)/shard_map/gmk,gkn->gmn/dot_general | solution.py:18
  206.2 3.6 %multiply_reduce_fusion.3 = (f32[4,128]{1,0:T(4,128)S(1)}, f32[4,128,512]{2,1,0:T(8,128)}) fusion(bf16[4,512,512]{2,1,0:T(8,128)(2,1)} %bitcast.119, f32[4,128,512]{2,1,0:T(8,128)} %fusion.82, bf16[4,20,512]{2,1,0:T(8,128)(2,1)S(1)} %all-gather.1, s32[4,128]{1,0:T(4,128)S(1)} %get-tuple-element.12, bf16[4,128,512]{2,1,0:T(8,128)(2,1)S(1)} %multiply_convert_fusion.4), kind=kOutput, calls=%fused_computation.44 | convolution fusion | flops 279716352 | bytes 4804608 | tf_op jit(solution)/shard_map/gmk,gkn->gmn/dot_general | solution.py:18
  209.8 2.0 slice.77
  211.8 1.4 multiply_convert_fusion.3
  213.2 1.4 fusion.83
  214.6 3.6 %multiply_reduce_fusion.2 = (f32[4,128]{1,0:T(4,128)S(1)}, f32[4,128,512]{2,1,0:T(8,128)}) fusion(bf16[4,512,512]{2,1,0:T(8,128)(2,1)} %bitcast.120, f32[4,128,512]{2,1,0:T(8,128)} %fusion.83, bf16[4,20,512]{2,1,0:T(8,128)(2,1)S(1)} %all-gather.1, s32[4,128]{1,0:T(4,128)S(1)} %get-tuple-element.11, bf16[4,128,512]{2,1,0:T(8,128)(2,1)} %copy-done.3), kind=kOutput, calls=%fused_computation.42 | convolution fusion | flops 279716352 | bytes 4804608 | tf_op jit(solution)/shard_map/gmk,gkn->gmn/dot_general | solution.py:18
  218.3 1.4 multiply_convert_fusion.2
  219.7 0.8 copy-done.4
  220.5 3.1 %fusion.84 = f32[4,128,512]{2,1,0:T(8,128)} fusion(bf16[4,128,512]{2,1,0:T(8,128)(2,1)S(1)} %multiply_convert_fusion.2, bf16[4,512,512]{2,1,0:T(8,128)(2,1)} %bitcast.115), kind=kOutput, calls=%fused_computation.157 | convolution fusion | flops 268435456 | bytes 3670016 | tf_op jit(solution)/shard_map/gmk,gkn->gmn/dot_general | solution.py:18
  223.5 3.6 %multiply_reduce_fusion.1 = (f32[4,128]{1,0:T(4,128)S(1)}, f32[4,128,512]{2,1,0:T(8,128)}) fusion(bf16[4,512,512]{2,1,0:T(8,128)(2,1)} %bitcast.121, f32[4,128,512]{2,1,0:T(8,128)} %fusion.84, bf16[4,20,512]{2,1,0:T(8,128)(2,1)S(1)} %all-gather.1, s32[4,128]{1,0:T(4,128)S(1)} %get-tuple-element.10, bf16[4,128,512]{2,1,0:T(8,128)(2,1)} %copy-done.4), kind=kOutput, calls=%fused_computation.40 | convolution fusion | flops 279716352 | bytes 4804608 | tf_op jit(solution)/shard_map/gmk,gkn->gmn/dot_general | solution.py:18
  227.1 1.4 fusion.66
  228.5 1.3 fusion.67
  229.8 0.2 fusion.68
  230.0 0.3 fusion.69
  230.5 0.2 fusion.65
  230.7 17.5 %all-gather.13.cloned.1.call-done = bf16[32,64,512]{2,1,0:T(8,128)(2,1)} async-done(((bf16[1,64,512]{2,1,0:T(8,128)(2,1)}), bf16[32,64,512]{2,1,0:T(8,128)(2,1)}) %all-gather.13.cloned.1.call-update) | async-done | bytes 2097168 | tf_op jit(solution)/shard_map/all_gather | solution.py:62
  248.2 2.7 %fusion.3 = f32[4,1,256]{2,1,0:T(1,128)S(1)} fusion(bf16[4,512,512]{2,1,0:T(8,128)(2,1)} %bitcast.136, bf16[4,128,512]{2,1,0:T(8,128)(2,1)S(1)} %multiply_convert_fusion.1, bf16[4,128,512]{2,1,0:T(8,128)(2,1)} %slice.77, bf16[4,20,512]{2,1,0:T(8,128)(2,1)S(1)} %all-gather.1), kind=kOutput, calls=%fused_computation.14 | convolution fusion | flops 541065216 | bytes 3158016 | tf_op jit(solution)/shard_map/gmk,gk->gm/dot_general | solution.py:120
  251.2 0.6 gather_fusion.2
  251.9 0.6 subtract_abs_fusion
  (93 shorter events, 3.5 us)
Async XLA Ops:
  6.5 35.2 %copy-start = (bf16[64,16,1024]{2,1,0:T(8,128)(2,1)S(1)}, bf16[64,16,1024]{2,1,0:T(8,128)(2,1)}, u32[]{:S(2)}) copy-start(bf16[64,16,1024]{2,1,0:T(8,128)(2,1)} %param.16) | copy-start | bytes 6291460
  6.5 6.2 %copy-start.1 = (s32[64,21]{0,1:T(8,128)S(1)}, s32[64,21]{0,1:T(8,128)}, u32[]{:S(2)}) copy-start(s32[64,21]{0,1:T(8,128)} %param.18) | copy-start | bytes 16132
  6.5 68.0 %all-gather.7.cloned.1.call-start = ((), (), s32[]{:S(2)}) async-start(), calls=%async_computation | async-start | bytes 4325376 | tf_op jit(solution)/shard_map/all_gather | solution.py:62
  7.3 125.1 %all-gather.9.cloned.1.call-start = ((), (), s32[]{:S(2)}) async-start(), calls=%async_computation.1 | async-start | bytes 2162688 | tf_op jit(solution)/shard_map/all_gather | solution.py:62
  8.0 182.3 %all-gather.11.cloned.1.call-start = ((), (), s32[]{:S(2)}) async-start(), calls=%async_computation.2 | async-start | bytes 2162688 | tf_op jit(solution)/shard_map/all_gather | solution.py:62
  8.7 239.4 %all-gather.13.cloned.1.call-start = ((), (), s32[]{:S(2)}) async-start(), calls=%async_computation.3 | async-start | bytes 2162688 | tf_op jit(solution)/shard_map/all_gather | solution.py:62
  22.5 2.3 copy-start.7
  22.5 3.9 %copy-start.10 = (s32[64,1]{0,1:T(1,128)S(1)}, s32[64,1]{0,1:T(1,128)}, u32[]{:S(2)}) copy-start(s32[64,1]{0,1:T(1,128)} %param.22) | copy-start | bytes 772
  22.5 3.9 %copy-start.11 = (s32[64]{0:T(128)S(1)}, s32[64]{0:T(128)}, u32[]{:S(2)}) copy-start(s32[64]{0:T(128)} %param.20) | copy-start | bytes 772
  24.5 1.9 copy-start.8
  24.5 1.9 copy-start.13
  24.5 1.9 copy-start.14
  24.6 17.2 %copy-start.12 = (s32[64]{0:T(128)S(1)}, s32[64]{0:T(128)}, u32[]{:S(2)}) copy-start(s32[64]{0:T(128)} %param.19) | copy-start | bytes 772
  41.8 5.4 %copy-start.9 = (f32[64,16]{0,1:T(8,128)S(1)}, f32[64,16]{0,1:T(8,128)}, u32[]{:S(2)}) copy-start(f32[64,16]{0,1:T(8,128)} %param.17) | copy-start | bytes 12292
  78.9 114.9 %copy-start.5 = (bf16[4,256,512]{2,1,0:T(8,128)(2,1)}, bf16[4,256,512]{2,1,0:T(8,128)(2,1)S(1)}, u32[]{:S(2)}) copy-start(bf16[4,256,512]{2,1,0:T(8,128)(2,1)S(1)} %multiply_convert_fusion) | copy-start | bytes 3145732
  209.8 3.4 %copy-start.2 = (bf16[32,64,512]{2,1,0:T(8,128)(2,1)S(1)}, bf16[32,64,512]{2,1,0:T(8,128)(2,1)}, u32[]{:S(2)}) copy-start(bf16[32,64,512]{2,1,0:T(8,128)(2,1)} %all-gather.9.cloned.1.call-done) | copy-start | bytes 6291460
  213.2 1.4 copy-start.3
  219.7 0.8 copy-start.4
  227.1 3.2 %copy-start.6 = (f32[4,128,512]{2,1,0:T(8,128)S(1)}, f32[4,128,512]{2,1,0:T(8,128)}, u32[]{:S(2)}) copy-start(f32[4,128,512]{2,1,0:T(8,128)} %get-tuple-element.39) | copy-start | bytes 3145732
Sparse Core Ops, SparseCore 0:
  10.2 64.2 all-gather.6
  77.3 54.9 all-gather.8
  135.2 55.0 all-gather.10
  193.0 55.1 all-gather.12

commit v2 on v1

v2 whole, which is shorter than its diff:
```python
import functools
import math

import jax
import jax.numpy as jnp
from jax import lax
from jax.experimental import pallas as pl
from jax.experimental.pallas import tpu as pltpu
from jax.sharding import PartitionSpec as P

MOSTG = 32
CORES = 2
MESH = pl.DeviceIdType.MESH


discount = 0.997
epsilon = 1e-06


def rms_scale(values):
    return values * lax.rsqrt(jnp.mean(values * values, axis=-1, keepdims=True) + epsilon)


def ranks_within(owner, groups):
    member = (owner[:, None] == jnp.arange(groups, dtype=jnp.int32)[None, :]).astype(jnp.int32)
    earlier = jnp.cumsum(member, axis=0) - member
    return jnp.sum(earlier * member, axis=1)


def reward_part(rewards, lengths, nsteps, picks):
    position = jnp.arange(rewards.shape[1], dtype=jnp.int32)
    offset = position[None, None, :] - picks[:, :, None]
    inside = (
        (offset >= 0)
        & (offset < nsteps[:, None, None])
        & (position[None, None, :] < lengths[:, None, None])
    )
    power = discount ** jnp.maximum(offset, 0).astype(jnp.float32)
    return jnp.sum(jnp.where(inside, power, 0.0) * rewards[:, None, :], axis=2)


def chip_cycle(chips):
    side = max(d for d in range(1, math.isqrt(chips) + 1) if chips % d == 0)
    wide = chips // side
    if side % 2 or wide < 2:
        return list(range(chips))
    order = [0]
    for row in range(side):
        columns = range(1, wide) if row % 2 == 0 else range(wide - 1, 0, -1)
        order += [row * wide + column for column in columns]
    return order + [row * wide for row in range(side - 1, 0, -1)]


def lookup(table, index):
    found = jnp.int32(table[0])
    for place in range(1, len(table)):
        found = jnp.where(index == place, jnp.int32(table[place]), found)
    return found


class Copies:
    def __init__(self, send, recv):
        self.send, self.recv, self.made = send, recv, []

    def start(self, source, target, device):
        k = len(self.made)
        copy = pltpu.make_async_remote_copy(
            src_ref=source,
            dst_ref=target,
            send_sem=self.send.at[k],
            recv_sem=self.recv.at[k],
            device_id=device,
            device_id_type=MESH,
        )
        copy.start()
        self.made.append(copy)
        return copy


def network_kernel(
    groups,
    shards,
    unroll,
    action_count,
    obs_ref,
    lines_ref,
    moves_ref,
    rep_ref,
    dyn_ref,
    val_ref,
    small_ref,
    out_ref,
    rep,
    dyn,
    val,
    small,
    latent,
    frames,
    total,
    send,
    recv,
    local,
):
    chips = shards // CORES
    half_ring, half_line = chips // 2, groups // 2
    me = lax.axis_index("replica")
    mine = lax.axis_index("shard")
    chip, core = mine // CORES, mine % CORES
    order = chip_cycle(chips)
    place = lookup([order.index(k) for k in range(chips)], chip)

    def at(distance):
        return lookup(order, lax.rem(place + distance + chips, chips))

    after, before = at(1), at(-1)
    up = (lax.rem(me + 1, groups), mine)
    down = (lax.rem(me + groups - 1, groups), mine)
    right = (me, after * CORES + core)
    left = (me, before * CORES + core)
    sibling = (me, chip * CORES + (1 - core))

    barrier = pltpu.get_barrier_semaphore()
    for device in (up, down, right, left, sibling):
        pl.semaphore_signal(barrier, inc=1, device_id=device, device_id_type=MESH)
    pl.semaphore_wait(barrier, 5)

    copies = Copies(send, recv)
    wide = rep_ref.shape[-1]
    halves = (pl.ds(0, wide // 2), pl.ds(wide // 2, wide // 2))

    def levels():
        return [(0, 1)] + [(2 * d - 1, 2) for d in range(1, half_line)] + [(groups - 1, 1)]

    def line(buffer, own, view, distance):
        pair = []
        for way, device in ((0, up), (1, down)):
            if distance == 1:
                source = own
            else:
                source = view(buffer.at[2 * (distance - 1) - 1 + way])
            last = distance == half_line
            slot = groups - 1 if last else 2 * distance - 1 + way
            target = view(buffer.at[slot])
            if last:
                source = source.at[(slice(None),) * (len(source.shape) - 1) + (halves[way],)]
                target = target.at[(slice(None),) * (len(target.shape) - 1) + (halves[way],)]
            pair.append(copies.start(source, target, device))
        return pair

    def ring(buffer, own, level, distance):
        first, count = level
        pair = []
        for way, device in ((0, right), (1, left)):
            origin = at((1 - distance) if way == 0 else (distance - 1))
            target = buffer.at[pl.ds(first, count), origin, core]
            source = own if own is not None and distance == 1 else target
            if own is not None and distance == 1:
                target = buffer.at[first, origin, core]
            if distance == half_ring:
                source = source.at[(slice(None),) * (len(source.shape) - 1) + (halves[way],)]
                target = target.at[(slice(None),) * (len(target.shape) - 1) + (halves[way],)]
            pair.append(copies.start(source, target, device))
        return pair

    def arrived(pair):
        for copy in pair:
            copy.wait_recv()

    def finish_ring(buffer, level, pair):
        for distance in range(2, half_ring + 1):
            arrived(pair)
            pair = ring(buffer, None, level, distance)
        return pair

    def share(buffer, level):
        first, count = level
        piece = buffer.at[pl.ds(first, count), :, core]
        return copies.start(piece, piece, sibling)

    def block(ref):
        return ref.at[chip, core]

    def plane(ref):
        return ref.at[:, core]

    def whole(ref):
        return ref

    own = []
    for k, (ref, buffer) in enumerate(((rep_ref, rep), (dyn_ref, dyn), (val_ref, val))):
        own.append(pltpu.make_async_copy(ref, buffer.at[0, chip, core], local.at[k]))
    own.append(pltpu.make_async_copy(small_ref, small.at[0], local.at[3]))
    for copy in own:
        copy.start()

    near, far = levels()[0], levels()[1:]
    rep_line = line(rep, rep_ref, block, 1)
    rep_ring = ring(rep, rep_ref, near, 1)
    small_line = line(small, small_ref, whole, 1)
    dyn_line = line(dyn, dyn_ref, block, 1)
    val_ring = ring(val, val_ref, near, 1)
    dyn_ring = ring(dyn, dyn_ref, near, 1)

    rows = lines_ref.shape[1]
    half = rows // 2
    observed = obs_ref.shape[0]

    def pick(slot, carry):
        one_hot = (
            lines_ref[slot] == lax.broadcasted_iota(jnp.int32, (rows, observed), 1)
        ).astype(jnp.bfloat16)
        frames[slot] = jnp.dot(
            one_hot, obs_ref[...], preferred_element_type=jnp.float32
        ).astype(jnp.bfloat16)
        return carry

    lax.fori_loop(0, groups, pick, 0)
    for copy in own:
        copy.wait()

    rep_far, dyn_far = [], []
    for index, level in enumerate(far):
        distance = index + 1
        arrived(rep_line)
        if distance < half_line:
            rep_line = line(rep, None, block, distance + 1)
        rep_far.append(ring(rep, None, level, 1))
        if index == 0:
            rep_ring = finish_ring(rep, near, rep_ring)
            val_ring = finish_ring(val, near, val_ring)
        arrived(small_line)
        if distance < half_line:
            small_line = line(small, None, whole, distance + 1)
        arrived(dyn_line)
        if distance < half_line:
            dyn_line = line(dyn, None, block, distance + 1)
        if index == 0:
            arrived(val_ring)
            val_line = line(val, val.at[0, :, core], plane, 1)
            dyn_ring = finish_ring(dyn, near, dyn_ring)
        dyn_far.append(ring(dyn, None, level, 1))
    shared = []
    for index, level in enumerate(far):
        rep_far[index] = finish_ring(rep, level, rep_far[index])
    arrived(rep_ring)
    rep_shared = [share(rep, near)]
    for index, level in enumerate(far):
        dyn_far[index] = finish_ring(dyn, level, dyn_far[index])
        arrived(rep_far[index])
        rep_shared.append(share(rep, level))
    arrived(dyn_ring)
    dyn_shared = [share(dyn, near)]
    val_shared = [share(val, near)]
    for distance in range(2, half_line + 1):
        arrived(val_line)
        val_line = line(val, None, plane, distance)
        val_shared.append(share(val, far[distance - 2]))
    arrived(rep_shared)

    def represent(slot, carry):
        weight = rep[slot].reshape(-1, wide)
        raw = jnp.dot(frames[slot], weight, preferred_element_type=jnp.float32)
        latent[slot] = rms_scale(raw).astype(jnp.bfloat16)
        return carry

    lax.fori_loop(0, groups, represent, 0)
    for index, level in enumerate(far):
        arrived(dyn_far[index])
        dyn_shared.append(share(dyn, level))
    arrived(dyn_shared)

    rows_in = dyn.shape[3] // 2
    total[...] = jnp.zeros_like(total)

    def advance(depth, scale):
        for slot in range(groups):
            first = dyn[slot, :, :, :rows_in].reshape(-1, wide)
            second = dyn[slot, :, :, rows_in:].reshape(-1, wide)
            table = small[slot]
            one_hot = (
                moves_ref[depth, slot]
                == lax.broadcasted_iota(jnp.int32, (half, table.shape[0]), 1)
            ).astype(jnp.bfloat16)
            state = latent[slot, half:]
            inner = jnp.maximum(
                jnp.dot(state, first, preferred_element_type=jnp.float32)
                + jnp.dot(one_hot, table, preferred_element_type=jnp.float32),
                0.0,
            ).astype(jnp.bfloat16)
            update = jnp.dot(inner, second, preferred_element_type=jnp.float32)
            state = rms_scale(state.astype(jnp.float32) + update).astype(jnp.bfloat16)
            latent[slot, half:] = state
            vector = table.astype(jnp.float32)[action_count + 1 : action_count + 2]
            guess = jnp.sum(state.astype(jnp.float32) * vector, axis=-1, keepdims=True)
            total[slot] = total[slot] + scale * guess
        return scale * discount

    lax.fori_loop(0, unroll, advance, jnp.float32(1.0))
    arrived(val_line)
    val_shared.append(share(val, far[-1]))
    arrived(val_shared)

    for slot in range(groups):
        weight = val[slot].reshape(-1, wide)
        hidden = jnp.maximum(
            jnp.dot(latent[slot], weight, preferred_element_type=jnp.float32), 0.0
        ).astype(jnp.bfloat16)
        vector = small[slot].astype(jnp.float32)[action_count : action_count + 1]
        value = jnp.sum(hidden.astype(jnp.float32) * vector, axis=-1, keepdims=True)
        model = total[slot] + discount**unroll * value[half:]
        lane = lax.broadcasted_iota(jnp.int32, (half, 2), 1)
        out_ref[slot] = jnp.where(lane == 0, value[:half], model)
    for copy in copies.made:
        copy.wait_send()


def copies_needed(groups, shards):
    chips = shards // CORES
    levels = 1 + groups // 2
    return 4 * groups + (2 * levels + 1) * chips + 3 * levels


def on_device(
    observations,
    rewards,
    actions,
    lengths,
    nsteps,
    prio_index,
    assignment,
    rep_weight,
    dyn_in,
    dyn_out,
    value_hidden,
    action_table,
    value_out,
    reward_out,
):
    groups = lax.axis_size("replica")
    batch, steps, width = observations.shape
    unroll = actions.shape[1] - steps
    picks = prio_index.shape[1]
    shards = lax.axis_size("shard")
    chips = shards // CORES
    me = lax.axis_index("replica")
    action_count = action_table.shape[1]
    hidden = rep_weight.shape[-1]
    small = jnp.concatenate([action_table[0], value_out, reward_out], axis=0)
    small = jnp.pad(small, ((0, -small.shape[0] % 32), (0, 0)))
    dyn = jnp.concatenate([dyn_in[0], dyn_out[0]], axis=0)

    owner = assignment[:, 0]
    ahead = (owner - me + groups) % groups
    slot_of = jnp.where(2 * ahead < groups, 2 * ahead, 2 * (groups - ahead) - 1)
    spot = slot_of * MOSTG + ranks_within(owner, groups)
    slots = groups * MOSTG
    match = spot[None, :] == jnp.arange(slots, dtype=jnp.int32)[:, None]
    source = jnp.sum(
        jnp.where(match, jnp.arange(batch, dtype=jnp.int32)[None, :], 0), axis=1
    )
    reach = prio_index + nsteps[:, None]
    alive = reach < lengths[:, None]
    reach = jnp.minimum(reach, steps - 1)
    base = jnp.arange(batch, dtype=jnp.int32)[:, None] * steps
    rows = jnp.concatenate([base + prio_index, base + reach], axis=1)
    moves = jnp.concatenate(
        [jnp.take_along_axis(actions, reach + depth, axis=1) for depth in range(unroll)], axis=1
    )
    packed = jnp.take(jnp.concatenate([rows, moves], axis=1), source, axis=0)
    packed = packed.reshape(groups, MOSTG, (2 + unroll), picks).transpose(0, 2, 1, 3)
    packed = packed.reshape(groups, 2 + unroll, MOSTG * picks)
    lines = packed[:, :2].reshape(groups, 2 * MOSTG * picks, 1)
    turns = packed[:, 2:].transpose(1, 0, 2)[..., None]
    rows = 2 * MOSTG * picks
    needed = copies_needed(groups, shards)

    def held(weight):
        return pltpu.VMEM((groups, chips, CORES) + weight.shape, weight.dtype)

    answered = pl.pallas_call(
        functools.partial(network_kernel, groups, shards, unroll, action_count),
        out_shape=jax.ShapeDtypeStruct((groups, rows // 2, 2), jnp.float32),
        in_specs=[pl.BlockSpec(memory_space=pltpu.VMEM)] * 7,
        out_specs=pl.BlockSpec(memory_space=pltpu.VMEM),
        scratch_shapes=[
            held(rep_weight[0]),
            held(dyn),
            held(value_hidden[0]),
            pltpu.VMEM((groups,) + small.shape, small.dtype),
            pltpu.VMEM((groups, rows, hidden), jnp.bfloat16),
            pltpu.VMEM((groups, rows, width), jnp.bfloat16),
            pltpu.VMEM((groups, rows // 2, 1), jnp.float32),
            pltpu.SemaphoreType.DMA((needed,)),
            pltpu.SemaphoreType.DMA((needed,)),
            pltpu.SemaphoreType.DMA((4,)),
        ],
        compiler_params=pltpu.CompilerParams(
            collective_id=0, has_side_effects=True, vmem_limit_bytes=56 * 1024 * 1024
        ),
    )(
        observations.reshape(batch * steps, width),
        lines,
        turns,
        rep_weight[0],
        dyn,
        value_hidden[0],
        small,
    )
    answered = answered.reshape(slots, picks * 2)
    back = jnp.take(answered, spot, axis=0).reshape(batch, picks, 2)
    bonus = discount ** nsteps.astype(jnp.float32)
    target = reward_part(rewards, lengths, nsteps, prio_index) + jnp.where(
        alive, bonus[:, None] * back[:, :, 1], 0.0
    )
    return jnp.abs(target - back[:, :, 0])


def solution(mesh):
    placed = (
        P(("replica", "shard"), None, None),
        P(("replica", "shard"), None),
        P(("replica", "shard"), None),
        P(("replica", "shard")),
        P(("replica", "shard")),
        P(("replica", "shard"), None),
        P(("replica", "shard"), None),
        P("replica", "shard", None),
        P("replica", "shard", None),
        P("replica", "shard", None),
        P("replica", "shard", None),
        P("replica", None, None),
        P("replica", None),
        P("replica", None),
    )
    return jax.shard_map(
        on_device,
        mesh=mesh,
        in_specs=placed,
        out_specs=P(("replica", "shard"), None),
        check_vma=False,
    )
```

time: 260 us -> 84.5 us (0.33)
  waiting for transfers between devices: 156 us -> 0 us
  Pallas kernels: 0 us -> 62 us
  matrix products: 41.7 us -> 0 us
  blocking collectives: 15.2 us -> 0 us
  between operations: 13.6 us -> 0.27 us
  other arithmetic: 9.86 us -> 3.2 us
  local copies, waits for them, and re-layouts: 22.7 us -> 17.9 us
    all_gather x4 -> x0, waiting for transfers between devices: 153 us -> none  [whole(): part = lax.all_gather(weight, both, axis=0, tiled=True)]
    pallas_call x0 -> x1, Pallas kernels: none -> 62 us  [on_device(): pl.pallas_call(functools.partial(network_kernel, groups, shards, unroll,...]
    dot_general x17 -> x0, matrix products: 41.7 us -> none  [the longest x11 35.7 us: matmul(): jnp.einsum('gmk,gkn->gmn', rows, weights, preferred_element_type=jnp.floa...]
    all_gather x1 -> x0, blocking collectives: 15.2 us -> none  [on_device(): small = lax.all_gather(small, 'replica', axis=0)]
    convert_element_type x6 -> x0, other arithmetic: 5.81 us -> none  [the longest x5 5.6 us: on_device(): rms_scale(state.astype(jnp.float32) + matmul(inner, full_out))]
    gather x3 -> x2, local copies, waits for them, and re-layouts: 6.01 us -> 0.66 us  [on_device(): back = jnp.take(answered, spot, axis=0).reshape(batch, picks, 2)]
    unnamed x4 -> x0, waiting for transfers between devices: 2.61 us -> none
  transfers between devices with their start and end apart: 4 -> 0, of which waited for: 4 -> 0; matrix products, arithmetic and copies ran while one was open for 27% -> 0% of each run, Pallas kernels for 0% -> 0%
where the time goes in v2:
time: 84.5 us; the launch traced here: 83.4 us
  Pallas kernels  62 us (73%)
  local copies, waits for them, and re-layouts  17.9 us (21%)
  other arithmetic  3.2 us (4%)
    pallas_call x1, Pallas kernels, on_device(): pl.pallas_call(functools.partial(network_kernel, groups, shards, unroll,...  62 us
    gather x25, local copies, waits for them, and re-layouts, on_device(): jnp.take_along_axis(actions, reach + depth, axis=1)  12 us

profile of v2, /device:TPU:0, one launch (start us, length us, event | category | flops | bytes accessed | tf_op | source)
XLA Modules:
  0.0 83.4 jit_solution(9297038616426595142)
XLA Ops:
  0.0 0.7 bitcast_or_fusion
  0.7 0.1 copy.54
  0.8 0.1 reshape.194
  0.9 2.0 %gather_fusion.2 = s32[256]{0:T(256)S(1)} fusion(s32[64,21]{0,1:T(8,128)S(1)} %copy-done, s32[256]{0:T(256)S(1)} %reshape.194), kind=kCustom, calls=%fused_computation.clone | custom fusion | bytes 4096 | tf_op jit(solution)/shard_map/jit(take_along_axis)/gather | solution.py:367
  3.0 0.1 reshape.197
  3.1 0.1 copy.55
  3.1 0.1 copy.56
  3.2 0.1 reshape.199
  3.4 2.0 %gather_fusion.3 = s32[256]{0:T(256)S(1)} fusion(s32[64,21]{0,1:T(8,128)S(1)} %copy-done, s32[256]{0:T(256)S(1)} %reshape.199), kind=kCustom, calls=%fused_computation.1.clone | custom fusion | bytes 4096 | tf_op jit(solution)/shard_map/jit(take_along_axis)/gather | solution.py:367
  5.4 0.1 reshape.202
  5.5 0.1 copy.57
  5.6 0.1 copy.58
  5.7 0.1 reshape.204
  5.8 2.0 %gather_fusion.4 = s32[256]{0:T(256)S(1)} fusion(s32[64,21]{0,1:T(8,128)S(1)} %copy-done, s32[256]{0:T(256)S(1)} %reshape.204), kind=kCustom, calls=%fused_computation.2.clone | custom fusion | bytes 4096 | tf_op jit(solution)/shard_map/jit(take_along_axis)/gather | solution.py:367
  7.8 0.1 reshape.207
  7.9 0.1 copy.59
  8.0 0.1 copy.60
  8.1 0.1 reshape.209
  8.2 2.0 %gather_fusion.5 = s32[256]{0:T(256)S(1)} fusion(s32[64,21]{0,1:T(8,128)S(1)} %copy-done, s32[256]{0:T(256)S(1)} %reshape.209), kind=kCustom, calls=%fused_computation.3.clone | custom fusion | bytes 4096 | tf_op jit(solution)/shard_map/jit(take_along_axis)/gather | solution.py:367
  10.2 0.1 reshape.212
  10.3 0.1 copy.61
  10.4 0.1 copy.62
  10.5 0.1 reshape.214
  10.6 0.0 copy-start.5
  10.6 2.0 %gather_fusion.6 = s32[256]{0:T(256)S(1)} fusion(s32[64,21]{0,1:T(8,128)S(1)} %copy-done, s32[256]{0:T(256)S(1)} %reshape.214), kind=kCustom, calls=%fused_computation.4.clone | custom fusion | bytes 4096 | tf_op jit(solution)/shard_map/jit(take_along_axis)/gather | solution.py:367
  12.7 0.1 reshape.217
  12.8 0.1 copy.63
  12.9 0.1 concatenate.9
  13.0 0.1 copy.64
  13.1 0.1 fusion.5
  13.2 0.1 reduce_window_sum.11
  13.3 0.2 select_reduce_fusion.1
  13.5 0.1 select_reduce_fusion
  13.6 0.6 gather_fusion
  14.2 0.1 copy.65
  14.3 0.1 gather.16
  14.4 0.1 reduce_sum.37
  14.5 0.2 copy.66
  14.8 0.3 reshape.115
  15.1 1.5 %copy.68.moves_ref = s32[5,4,128,1]{3,2,1,0:T(8,128)} copy(s32[5,4,128,1]{2,1,0,3:T(4,128)S(1)} %slice_bitcast_fusion) | data formatting | bytes 20480 | tf_op jit(solution)/shard_map/broadcast_in_dim | solution.py:373
  16.6 1.1 %copy.67.lines_ref = s32[4,256,1]{2,1,0:T(8,128)} copy(s32[4,256,1]{1,0,2:T(4,128)S(1)} %slice_bitcast_fusion.1) | data formatting | bytes 8192 | tf_op jit(solution)/shard_map/reshape | solution.py:372
  17.6 0.7 pad_maximum_fusion.dyn_ref
  18.3 0.6 fusion.4.small_ref
  18.9 62.0 %shard_map.136 = f32[4,128,2]{2,1,0:T(8,128)} custom-call(bf16[1024,1024]{1,0:T(8,128)(2,1)} %bitcast.71, s32[4,256,1]{2,1,0:T(8,128)} %copy.67.lines_ref, s32[5,4,128,1]{3,2,1,0:T(8,128)} %copy.68.moves_ref, bf16[128,512]{1,0:T(8,128)(2,1)} %bitcast.72, bf16[128,512]{1,0:T(8,128)(2,1)} %pad_maximum_fusion.dyn_ref, bf16[64,512]{1,0:T(8,128)(2,1)} %bitcast.73, ...), custom_call_target="tpu_custom_call" | custom-call | tf_op jit(solution)/shard_map/pallas_call | solution.py:380
  80.9 1.1 %reshape.117 = f32[128,8]{1,0:T(8,128)S(1)} reshape(f32[4,128,2]{2,1,0:T(8,128)} %shard_map.136) | data formatting | bytes 8192 | tf_op jit(solution)/shard_map/reshape | solution.py:409
  82.0 0.6 gather_fusion.1
  82.6 0.1 copy.69
  82.8 0.6 fusion.11
  (37 shorter events, 0.2 us)
Async XLA Ops:
  0.0 0.9 %copy-start = (s32[64,21]{0,1:T(8,128)S(1)}, s32[64,21]{0,1:T(8,128)}, u32[]{:S(2)}) copy-start(s32[64,21]{0,1:T(8,128)} %param.18) | copy-start | bytes 16132
  10.6 2.3 %copy-start.3 = (s32[64,4]{0,1:T(4,128)S(1)}, s32[64,4]{0,1:T(4,128)}, u32[]{:S(2)}) copy-start(s32[64,4]{0,1:T(4,128)} %param.21) | copy-start | bytes 3076
  10.6 2.5 %copy-start.5 = (s32[64,1]{0,1:T(1,128)S(1)}, s32[64,1]{0,1:T(1,128)}, u32[]{:S(2)}) copy-start(s32[64,1]{0,1:T(1,128)} %param.22) | copy-start | bytes 772
  12.7 5.0 %copy-start.1 = (bf16[1,64,512]{2,1,0:T(8,128)(2,1)S(1)}, bf16[1,64,512]{2,1,0:T(8,128)(2,1)}, u32[]{:S(2)}) copy-start(bf16[1,64,512]{2,1,0:T(8,128)(2,1)} %param.25) | copy-start | bytes 196612
  12.7 4.9 %copy-start.2 = (bf16[1,64,512]{2,1,0:T(8,128)(2,1)S(1)}, bf16[1,64,512]{2,1,0:T(8,128)(2,1)}, u32[]{:S(2)}) copy-start(bf16[1,64,512]{2,1,0:T(8,128)(2,1)} %param.24) | copy-start | bytes 196612
  13.0 5.3 %copy-start.4 = (bf16[1,18,512]{2,1,0:T(8,128)(2,1)S(1)}, bf16[1,18,512]{2,1,0:T(8,128)(2,1)}, u32[]{:S(2)}) copy-start(bf16[1,18,512]{2,1,0:T(8,128)(2,1)} %param.27) | copy-start | bytes 55300
  13.0 5.3 %copy-start.8 = (bf16[1,512]{1,0:T(2,128)(2,1)S(1)}, bf16[1,512]{1,0:T(2,128)(2,1)}, u32[]{:S(2)}) copy-start(bf16[1,512]{1,0:T(2,128)(2,1)} %param.29) | copy-start | bytes 3076
  13.0 5.3 %copy-start.9 = (bf16[1,512]{1,0:T(2,128)(2,1)S(1)}, bf16[1,512]{1,0:T(2,128)(2,1)}, u32[]{:S(2)}) copy-start(bf16[1,512]{1,0:T(2,128)(2,1)} %param.28) | copy-start | bytes 3076
  18.9 63.8 %copy-start.10 = (s32[64]{0:T(128)S(1)}, s32[64]{0:T(128)}, u32[]{:S(2)}) copy-start(s32[64]{0:T(128)} %param.19) | copy-start | bytes 772
  18.9 63.8 %copy-start.6 = (f32[64,16]{0,1:T(8,128)S(1)}, f32[64,16]{0,1:T(8,128)}, u32[]{:S(2)}) copy-start(f32[64,16]{0,1:T(8,128)} %param.17) | copy-start | bytes 12292
  18.9 63.8 %copy-start.7 = (s32[64]{0:T(128)S(1)}, s32[64]{0:T(128)}, u32[]{:S(2)}) copy-start(s32[64]{0:T(128)} %param.20) | copy-start | bytes 772

commit v3 on v2

--- a/solution.py
+++ b/solution.py
@@ -82,14 +82,18 @@
     shards,
     unroll,
     action_count,
-    obs_ref,
-    lines_ref,
-    moves_ref,
+    obs_hbm,
+    key_ref,
+    acts_ref,
+    spot_ref,
     rep_ref,
-    dyn_ref,
+    in_ref,
+    back_ref,
     val_ref,
     small_ref,
     out_ref,
+    obs_ref,
+    moves_ref,
     rep,
     dyn,
     val,
@@ -186,37 +190,55 @@
     def whole(ref):
         return ref
 
-    own = []
-    for k, (ref, buffer) in enumerate(((rep_ref, rep), (dyn_ref, dyn), (val_ref, val))):
-        own.append(pltpu.make_async_copy(ref, buffer.at[0, chip, core], local.at[k]))
-    own.append(pltpu.make_async_copy(small_ref, small.at[0], local.at[3]))
-    for copy in own:
-        copy.start()
+    rows_in = dyn.shape[3] // 2
+    mine_dyn = dyn.at[0, chip, core]
+    own = [
+        pltpu.make_async_copy(in_ref, mine_dyn.at[pl.ds(0, rows_in)], local.at[0]),
+        pltpu.make_async_copy(back_ref, mine_dyn.at[pl.ds(rows_in, rows_in)], local.at[1]),
+        pltpu.make_async_copy(rep_ref, rep.at[0, chip, core], local.at[2]),
+        pltpu.make_async_copy(val_ref, val.at[0, chip, core], local.at[3]),
+        pltpu.make_async_copy(small_ref, small.at[0], local.at[4]),
+        pltpu.make_async_copy(obs_hbm, obs_ref, local.at[5]),
+    ]
 
     near, far = levels()[0], levels()[1:]
     rep_line = line(rep, rep_ref, block, 1)
     rep_ring = ring(rep, rep_ref, near, 1)
+    for copy in own:
+        copy.start()
     small_line = line(small, small_ref, whole, 1)
-    dyn_line = line(dyn, dyn_ref, block, 1)
     val_ring = ring(val, val_ref, near, 1)
-    dyn_ring = ring(dyn, dyn_ref, near, 1)
-
-    rows = lines_ref.shape[1]
-    half = rows // 2
+    own[0].wait()
+    own[1].wait()
+    dyn_line = line(dyn, mine_dyn, block, 1)
+    dyn_ring = ring(dyn, None, near, 1)
+    for copy in own[2:]:
+        copy.wait()
+
+    kinds = key_ref.shape[0]
+    most = frames.shape[1] // kinds
+    picks = kinds // 2
+    half = picks * most
     observed = obs_ref.shape[0]
 
     def pick(slot, carry):
-        one_hot = (
-            lines_ref[slot] == lax.broadcasted_iota(jnp.int32, (rows, observed), 1)
-        ).astype(jnp.bfloat16)
+        rank = slot * most + lax.broadcasted_iota(jnp.int32, (most, observed), 0)
+        one_hot = jnp.concatenate(
+            [
+                jnp.where(key_ref[kind : kind + 1] == rank, 1.0, 0.0).astype(jnp.bfloat16)
+                for kind in range(kinds)
+            ],
+            axis=0,
+        )
         frames[slot] = jnp.dot(
             one_hot, obs_ref[...], preferred_element_type=jnp.float32
         ).astype(jnp.bfloat16)
+        moves_ref[slot] = jnp.dot(
+            one_hot[half:], acts_ref[...], preferred_element_type=jnp.float32
+        )
         return carry
 
     lax.fori_loop(0, groups, pick, 0)
-    for copy in own:
-        copy.wait()
 
     rep_far, dyn_far = [], []
     for index, level in enumerate(far):
@@ -239,67 +261,89 @@
             val_line = line(val, val.at[0, :, core], plane, 1)
             dyn_ring = finish_ring(dyn, near, dyn_ring)
         dyn_far.append(ring(dyn, None, level, 1))
-    shared = []
+
+    def represent(level):
+        for slot in range(level[0], level[0] + level[1]):
+            weight = rep[slot].reshape(-1, wide)
+            raw = jnp.dot(frames[slot], weight, preferred_element_type=jnp.float32)
+            latent[slot] = rms_scale(raw).astype(jnp.bfloat16)
+
+    def unrolled(level):
+        slots = range(level[0], level[0] + level[1])
+        lane = lax.broadcasted_iota(jnp.int32, (half, moves_ref.shape[-1]), 1)
+
+        def advance(depth, carry):
+            scale, totals = carry
+            grown = []
+            for slot, so_far in zip(slots, totals):
+                first = dyn[slot, :, :, :rows_in].reshape(-1, wide)
+                second = dyn[slot, :, :, rows_in:].reshape(-1, wide)
+                table = small[slot]
+                move = jnp.sum(
+                    jnp.where(lane == depth, moves_ref[slot], 0.0), axis=-1, keepdims=True
+                ).astype(jnp.int32)
+                one_hot = jnp.where(
+                    move == lax.broadcasted_iota(jnp.int32, (half, table.shape[0]), 1), 1.0, 0.0
+                ).astype(jnp.bfloat16)
+                state = latent[slot, half:]
+                inner = jnp.maximum(
+                    jnp.dot(state, first, preferred_element_type=jnp.float32)
+                    + jnp.dot(one_hot, table, preferred_element_type=jnp.float32),
+                    0.0,
+                ).astype(jnp.bfloat16)
+                update = jnp.dot(inner, second, preferred_element_type=jnp.float32)
+                state = rms_scale(state.astype(jnp.float32) + update).astype(jnp.bfloat16)
+                latent[slot, half:] = state
+                vector = table.astype(jnp.float32)[action_count + 1 : action_count + 2]
+                guess = jnp.sum(state.astype(jnp.float32) * vector, axis=-1, keepdims=True)
+                grown.append(so_far + scale * guess)
+            return scale * discount, tuple(grown)
+
+        zeros = tuple(jnp.zeros((half, 1), jnp.float32) for _ in slots)
+        _, totals = lax.fori_loop(0, unroll, advance, (jnp.float32(1.0), zeros))
+        for slot, so_far in zip(slots, totals):
+            total[slot] = so_far
+
     for index, level in enumerate(far):
         rep_far[index] = finish_ring(rep, level, rep_far[index])
     arrived(rep_ring)
     rep_shared = [share(rep, near)]
-    for index, level in enumerate(far):
+    dyn_far[0] = finish_ring(dyn, far[0], dyn_far[0])
+    arrived(rep_far[0])
+    rep_shared.append(share(rep, far[0]))
+    arrived(dyn_ring)
+    dyn_shared = [share(dyn, near)]
+    val_shared = [share(val, near)]
+    arrived(rep_shared[:1])
+    represent(near)
+    for index, level in list(enumerate(far))[1:]:
         dyn_far[index] = finish_ring(dyn, level, dyn_far[index])
         arrived(rep_far[index])
         rep_shared.append(share(rep, level))
-    arrived(dyn_ring)
-    dyn_shared = [share(dyn, near)]
-    val_shared = [share(val, near)]
     for distance in range(2, half_line + 1):
         arrived(val_line)
         val_line = line(val, None, plane, distance)
         val_shared.append(share(val, far[distance - 2]))
-    arrived(rep_shared)
-
-    def represent(slot, carry):
-        weight = rep[slot].reshape(-1, wide)
-        raw = jnp.dot(frames[slot], weight, preferred_element_type=jnp.float32)
-        latent[slot] = rms_scale(raw).astype(jnp.bfloat16)
-        return carry
-
-    lax.fori_loop(0, groups, represent, 0)
+    for index, level in enumerate(far[:-1]):
+        arrived(rep_shared[index + 1 : index + 2])
+        represent(level)
+    arrived(dyn_shared[:1])
+    unrolled(near)
     for index, level in enumerate(far):
         arrived(dyn_far[index])
         dyn_shared.append(share(dyn, level))
-    arrived(dyn_shared)
-
-    rows_in = dyn.shape[3] // 2
-    total[...] = jnp.zeros_like(total)
-
-    def advance(depth, scale):
-        for slot in range(groups):
-            first = dyn[slot, :, :, :rows_in].reshape(-1, wide)
-            second = dyn[slot, :, :, rows_in:].reshape(-1, wide)
-            table = small[slot]
-            one_hot = (
-                moves_ref[depth, slot]
-                == lax.broadcasted_iota(jnp.int32, (half, table.shape[0]), 1)
-            ).astype(jnp.bfloat16)
-            state = latent[slot, half:]
-            inner = jnp.maximum(
-                jnp.dot(state, first, preferred_element_type=jnp.float32)
-                + jnp.dot(one_hot, table, preferred_element_type=jnp.float32),
-                0.0,
-            ).astype(jnp.bfloat16)
-            update = jnp.dot(inner, second, preferred_element_type=jnp.float32)
-            state = rms_scale(state.astype(jnp.float32) + update).astype(jnp.bfloat16)
-            latent[slot, half:] = state
-            vector = table.astype(jnp.float32)[action_count + 1 : action_count + 2]
-            guess = jnp.sum(state.astype(jnp.float32) * vector, axis=-1, keepdims=True)
-            total[slot] = total[slot] + scale * guess
-        return scale * discount
-
-    lax.fori_loop(0, unroll, advance, jnp.float32(1.0))
+    arrived(rep_shared[-1:])
+    represent(far[-1])
+    for index, level in enumerate(far[:-1]):
+        arrived(dyn_shared[index + 1 : index + 2])
+        unrolled(level)
     arrived(val_line)
     val_shared.append(share(val, far[-1]))
+    arrived(dyn_shared[-1:])
+    unrolled(far[-1])
     arrived(val_shared)
 
+    answers = [0.0] * kinds
     for slot in range(groups):
         weight = val[slot].reshape(-1, wide)
         hidden = jnp.maximum(
@@ -308,8 +352,13 @@
         vector = small[slot].astype(jnp.float32)[action_count : action_count + 1]
         value = jnp.sum(hidden.astype(jnp.float32) * vector, axis=-1, keepdims=True)
         model = total[slot] + discount**unroll * value[half:]
-        lane = lax.broadcasted_iota(jnp.int32, (half, 2), 1)
-        out_ref[slot] = jnp.where(lane == 0, value[:half], model)
+        rank = slot * most + lax.broadcasted_iota(jnp.int32, (most, spot_ref.shape[1]), 0)
+        here = spot_ref[...] == rank
+        for kind in range(kinds):
+            source = value if kind < picks else model
+            part = source[kind % picks * most : (kind % picks + 1) * most]
+            answers[kind] += jnp.sum(jnp.where(here, part, 0.0), axis=0, keepdims=True)
+    out_ref[...] = jnp.concatenate(answers, axis=0)
     for copy in copies.made:
         copy.wait_send()
 
@@ -347,72 +396,67 @@
     hidden = rep_weight.shape[-1]
     small = jnp.concatenate([action_table[0], value_out, reward_out], axis=0)
     small = jnp.pad(small, ((0, -small.shape[0] % 32), (0, 0)))
-    dyn = jnp.concatenate([dyn_in[0], dyn_out[0]], axis=0)
 
     owner = assignment[:, 0]
     ahead = (owner - me + groups) % groups
     slot_of = jnp.where(2 * ahead < groups, 2 * ahead, 2 * (groups - ahead) - 1)
     spot = slot_of * MOSTG + ranks_within(owner, groups)
-    slots = groups * MOSTG
-    match = spot[None, :] == jnp.arange(slots, dtype=jnp.int32)[:, None]
-    source = jnp.sum(
-        jnp.where(match, jnp.arange(batch, dtype=jnp.int32)[None, :], 0), axis=1
-    )
     reach = prio_index + nsteps[:, None]
     alive = reach < lengths[:, None]
     reach = jnp.minimum(reach, steps - 1)
-    base = jnp.arange(batch, dtype=jnp.int32)[:, None] * steps
-    rows = jnp.concatenate([base + prio_index, base + reach], axis=1)
-    moves = jnp.concatenate(
-        [jnp.take_along_axis(actions, reach + depth, axis=1) for depth in range(unroll)], axis=1
-    )
-    packed = jnp.take(jnp.concatenate([rows, moves], axis=1), source, axis=0)
-    packed = packed.reshape(groups, MOSTG, (2 + unroll), picks).transpose(0, 2, 1, 3)
-    packed = packed.reshape(groups, 2 + unroll, MOSTG * picks)
-    lines = packed[:, :2].reshape(groups, 2 * MOSTG * picks, 1)
-    turns = packed[:, 2:].transpose(1, 0, 2)[..., None]
+    wanted = jnp.concatenate([prio_index, reach], axis=1).T
+    step = jnp.arange(steps, dtype=jnp.int32)
+    key = jnp.where(wanted[:, :, None] == step[None, None, :], spot[None, :, None], -1)
+    key = key.reshape(2 * picks, batch * steps)
+    acts = jnp.stack([actions[:, depth : depth + steps] for depth in range(unroll)], axis=2)
+    acts = acts.astype(jnp.bfloat16).reshape(batch * steps, unroll)
+    acts = jnp.pad(acts, ((0, 0), (0, -unroll % 128)))
     rows = 2 * MOSTG * picks
     needed = copies_needed(groups, shards)
 
-    def held(weight):
-        return pltpu.VMEM((groups, chips, CORES) + weight.shape, weight.dtype)
+    def held(count):
+        return pltpu.VMEM((groups, chips, CORES, count, hidden), jnp.bfloat16)
 
     answered = pl.pallas_call(
         functools.partial(network_kernel, groups, shards, unroll, action_count),
-        out_shape=jax.ShapeDtypeStruct((groups, rows // 2, 2), jnp.float32),
-        in_specs=[pl.BlockSpec(memory_space=pltpu.VMEM)] * 7,
+        out_shape=jax.ShapeDtypeStruct((2 * picks, batch), jnp.float32),
+        in_specs=[pl.BlockSpec(memory_space=pl.ANY)]
+        + [pl.BlockSpec(memory_space=pltpu.VMEM)] * 8,
         out_specs=pl.BlockSpec(memory_space=pltpu.VMEM),
         scratch_shapes=[
-            held(rep_weight[0]),
-            held(dyn),
-            held(value_hidden[0]),
+            pltpu.VMEM((batch * steps, width), jnp.bfloat16),
+            pltpu.VMEM((groups, rows // 2, acts.shape[1]), jnp.float32),
+            held(rep_weight.shape[1]),
+            held(dyn_in.shape[1] + dyn_out.shape[1]),
+            held(value_hidden.shape[1]),
             pltpu.VMEM((groups,) + small.shape, small.dtype),
             pltpu.VMEM((groups, rows, hidden), jnp.bfloat16),
             pltpu.VMEM((groups, rows, width), jnp.bfloat16),
             pltpu.VMEM((groups, rows // 2, 1), jnp.float32),
             pltpu.SemaphoreType.DMA((needed,)),
             pltpu.SemaphoreType.DMA((needed,)),
-            pltpu.SemaphoreType.DMA((4,)),
+            pltpu.SemaphoreType.DMA((6,)),
         ],
         compiler_params=pltpu.CompilerParams(
             collective_id=0, has_side_effects=True, vmem_limit_bytes=56 * 1024 * 1024
         ),
     )(
         observations.reshape(batch * steps, width),
-        lines,
-        turns,
+        key,
+        acts,
+        spot[None, :],
         rep_weight[0],
-        dyn,
+        dyn_in[0],
+        dyn_out[0],
         value_hidden[0],
         small,
     )
-    answered = answered.reshape(slots, picks * 2)
-    back = jnp.take(answered, spot, axis=0).reshape(batch, picks, 2)
+    root_value, model_return = answered[:picks].T, answered[picks:].T
     bonus = discount ** nsteps.astype(jnp.float32)
     target = reward_part(rewards, lengths, nsteps, prio_index) + jnp.where(
-        alive, bonus[:, None] * back[:, :, 1], 0.0
+        alive, bonus[:, None] * model_return, 0.0
     )
-    return jnp.abs(target - back[:, :, 0])
+    return jnp.abs(target - root_value)
 
 
 def solution(mesh):

time: 84.5 us -> 74.7 us (0.88)
  local copies, waits for them, and re-layouts: 17.9 us -> 2.51 us
  other arithmetic: 3.2 us -> 10.4 us
    gather x30 -> x0, local copies, waits for them, and re-layouts: 13.5 us -> none  [the longest x25 12 us: on_device(): jnp.take_along_axis(actions, reach + depth, axis=1)]
    reshape x4 -> x0, local copies, waits for them, and re-layouts: 2.38 us -> none  [the longest x1 1.06 us: on_device(): answered = answered.reshape(slots, picks * 2)]
    add x1 -> x2, other arithmetic: 0.02 us -> 1.86 us  [on_device(): spot = slot_of * MOSTG + ranks_within(owner, groups)]
    broadcast_in_dim x2, local copies, waits for them, and re-layouts: 1.51 us -> 0.15 us  [on_device(): jnp.where(wanted[:, :, None] == step[None, None, :], spot[None, :, None],...]
where the time goes in v3:
time: 74.7 us; the launch traced here: 74.3 us
  Pallas kernels  61.2 us (82%)
  other arithmetic  10.4 us (14%)
  local copies, waits for them, and re-layouts  2.51 us (3%)
    pallas_call x1, Pallas kernels, on_device(): pl.pallas_call(functools.partial(network_kernel, groups, shards, unroll,...  61.2 us
    add x2, other arithmetic, on_device(): spot = slot_of * MOSTG + ranks_within(owner, groups)  1.86 us

profile of v3, /device:TPU:0, one launch (start us, length us, event | category | flops | bytes accessed | tf_op | source)
XLA Modules:
  0.0 74.3 jit_solution(13165972175835645495)
XLA Ops:
  0.0 0.7 iota_compare_fusion.2
  0.7 0.8 %multiply_reduce_fusion = f32[64,4]{0,1:T(4,128)S(1)} fusion(f32[64,16]{0,1:T(8,128)} %param.15, s32[64]{0:T(128)} %param.18, s32[64,4]{0,1:T(4,128)} %param.19, pred[64,16]{0,1:T(8,128)(4,1)S(1)} %iota_compare_fusion.2), kind=kLoop, calls=%fused_computation.9 | loop fusion | flops 40704 | bytes 7424 | tf_op jit(solution)/shard_map/reduce_sum | solution.py:39
  1.4 0.7 add_minimum_fusion
  2.1 0.7 add_bitcast_fusion
  2.8 0.1 eq.35
  2.9 0.2 eq.36
  3.1 0.7 fusion.5
  3.8 0.1 reduce_window_sum.11
  3.9 0.0 copy-start.1
  3.9 0.0 copy-start
  3.9 0.0 copy-start.2
  3.9 0.9 %select_reduce_fusion = s32[64]{0:T(128)S(1)} fusion(s32[64,4]{1,0:T(8,128)S(1)} %reduce_window_sum.11, s32[64]{0:T(128)} %bitcast.33), kind=kLoop, calls=%fused_computation.6 | loop fusion | flops 1216 | bytes 1536 | tf_op jit(solution)/shard_map/reduce_sum | solution.py:27
  4.8 0.7 fusion.15
  5.5 0.1 broadcast_in_dim.24
  5.6 0.1 broadcast_in_dim.40
  5.6 0.1 eq.38
  5.7 0.6 compare_select_fusion.key_ref
  6.3 0.7 convert.17
  7.1 0.1 copy.42
  7.2 0.1 stack.18
  7.2 0.1 copy.43
  7.3 0.1 stack.19
  7.4 0.1 copy.44
  7.5 0.1 stack.20
  7.6 0.1 copy.45
  7.7 0.1 stack.21
  7.8 0.1 copy.46
  7.9 0.1 stack.22
  8.1 0.2 copy.47
  8.3 0.8 %pad.8.acts_ref = bf16[1024,128]{1,0:T(8,128)(2,1)} pad(bf16[1024,5]{1,0:T(8,128)(2,1)S(1)} %copy.47, bf16[]{:T(256)} %constant.45.clone.1), padding=0_0x0_123 | pad | bytes 272386 | tf_op jit(solution)/shard_map/jit(_pad)/pad | solution.py:413
  9.0 1.2 %fusion.17.spot_ref = s32[1,64]{1,0:T(1,128)} fusion(s32[64]{0:T(128)S(1)} %select_reduce_fusion, s32[64,1]{0,1:T(1,128)} %param.20, s32[]{:T(128)S(6)} %axis_index.15), kind=kLoop, calls=%fused_computation.36 | loop fusion | flops 1344 | bytes 772 | tf_op jit(solution)/shard_map/add | solution.py:403
  10.2 1.4 %fusion.4.small_ref = bf16[32,512]{1,0:T(8,128)(2,1)} fusion(bf16[1,512]{1,0:T(2,128)(2,1)} %param.27, bf16[1,512]{1,0:T(2,128)(2,1)} %param.26, bf16[18,512]{1,0:T(8,128)(2,1)} %bitcast.31), kind=kLoop, calls=%fused_computation.5 | loop fusion | flops 163840 | bytes 53248 | tf_op jit(solution)/shard_map/concatenate | solution.py:397
  11.6 61.2 %shard_map.136 = f32[8,64]{1,0:T(8,128)} custom-call(bf16[1024,1024]{1,0:T(8,128)(2,1)} %bitcast.26, s32[8,1024]{1,0:T(8,128)} %compare_select_fusion.key_ref, bf16[1024,128]{1,0:T(8,128)(2,1)} %pad.8.acts_ref, s32[1,64]{1,0:T(1,128)} %fusion.17.spot_ref, bf16[128,512]{1,0:T(8,128)(2,1)} %bitcast.27, bf16[64,512]{1,0:T(8,128)(2,1)} %bitcast.28, ...), custom_call_target="tpu_custom_call" | custom-call | tf_op jit(solution)/shard_map/pallas_call | solution.py:420
  72.9 0.0 copy-done.1
  72.9 0.0 copy-done
  72.9 0.0 copy-done.2
  72.9 1.3 %fusion.10 = f32[64,4]{0,1:T(4,128)} fusion(f32[64,4]{0,1:T(4,128)S(1)} %multiply_reduce_fusion, f32[8,64]{1,0:T(8,128)} %shard_map.136, s32[64,4]{0,1:T(4,128)S(1)} %copy-done, f32[64]{0:T(128)S(1)} %convert_power_fusion, s32[64]{0:T(128)S(1)} %copy-done.2, s32[64]{0:T(128)S(1)} %copy-done.1), kind=kLoop, calls=%fused_computation.25 | loop fusion | flops 1792 | bytes 5888 | tf_op jit(solution)/shard_map/abs | solution.py:459
  (4 shorter events, 0.1 us)
Async XLA Ops:
  3.9 69.0 %copy-start.1 = (s32[64]{0:T(128)S(1)}, s32[64]{0:T(128)}, u32[]{:S(2)}) copy-start(s32[64]{0:T(128)} %param.18) | copy-start | bytes 772
  3.9 69.0 %copy-start = (s32[64,4]{0,1:T(4,128)S(1)}, s32[64,4]{0,1:T(4,128)}, u32[]{:S(2)}) copy-start(s32[64,4]{0,1:T(4,128)} %param.19) | copy-start | bytes 3076
  3.9 69.0 %copy-start.2 = (s32[64]{0:T(128)S(1)}, s32[64]{0:T(128)}, u32[]{:S(2)}) copy-start(s32[64]{0:T(128)} %param.17) | copy-start | bytes 772

commit v4 on v3

--- a/solution.py
+++ b/solution.py
@@ -21,10 +21,10 @@
     return values * lax.rsqrt(jnp.mean(values * values, axis=-1, keepdims=True) + epsilon)
 
 
-def ranks_within(owner, groups):
-    member = (owner[:, None] == jnp.arange(groups, dtype=jnp.int32)[None, :]).astype(jnp.int32)
-    earlier = jnp.cumsum(member, axis=0) - member
-    return jnp.sum(earlier * member, axis=1)
+def ranks_within(owner):
+    place = jnp.arange(owner.shape[0], dtype=jnp.int32)
+    earlier = (owner[None, :] == owner[:, None]) & (place[None, :] < place[:, None])
+    return jnp.sum(earlier.astype(jnp.int32), axis=1)
 
 
 def reward_part(rewards, lengths, nsteps, picks):
@@ -320,27 +320,24 @@
         dyn_far[index] = finish_ring(dyn, level, dyn_far[index])
         arrived(rep_far[index])
         rep_shared.append(share(rep, level))
-    for distance in range(2, half_line + 1):
-        arrived(val_line)
-        val_line = line(val, None, plane, distance)
-        val_shared.append(share(val, far[distance - 2]))
     for index, level in enumerate(far[:-1]):
         arrived(rep_shared[index + 1 : index + 2])
         represent(level)
     arrived(dyn_shared[:1])
     unrolled(near)
+    for distance in range(2, half_line + 1):
+        arrived(val_line)
+        val_line = line(val, None, plane, distance)
+        val_shared.append(share(val, far[distance - 2]))
     for index, level in enumerate(far):
         arrived(dyn_far[index])
         dyn_shared.append(share(dyn, level))
     arrived(rep_shared[-1:])
     represent(far[-1])
-    for index, level in enumerate(far[:-1]):
-        arrived(dyn_shared[index + 1 : index + 2])
-        unrolled(level)
+    arrived(dyn_shared[1:])
+    unrolled((1, groups - 1))
     arrived(val_line)
     val_shared.append(share(val, far[-1]))
-    arrived(dyn_shared[-1:])
-    unrolled(far[-1])
     arrived(val_shared)
 
     answers = [0.0] * kinds
@@ -400,7 +397,7 @@
     owner = assignment[:, 0]
     ahead = (owner - me + groups) % groups
     slot_of = jnp.where(2 * ahead < groups, 2 * ahead, 2 * (groups - ahead) - 1)
-    spot = slot_of * MOSTG + ranks_within(owner, groups)
+    spot = slot_of * MOSTG + ranks_within(owner)
     reach = prio_index + nsteps[:, None]
     alive = reach < lengths[:, None]
     reach = jnp.minimum(reach, steps - 1)

time: 74.7 us -> 74.5 us (level)
  other arithmetic: 10.4 us -> 9.61 us
where the time goes in v4:
time: 74.5 us; the launch traced here: 73.3 us
  Pallas kernels  61.1 us (82%)
  other arithmetic  9.61 us (13%)
  local copies, waits for them, and re-layouts  2.52 us (3%)
    pallas_call x1, Pallas kernels, on_device(): pl.pallas_call(functools.partial(network_kernel, groups, shards, unroll,...  61.1 us
    add x2, other arithmetic, on_device(): spot = slot_of * MOSTG + ranks_within(owner)  1.86 us

profile of v4, /device:TPU:0, one launch (start us, length us, event | category | flops | bytes accessed | tf_op | source)
XLA Modules:
  0.0 73.3 jit_solution(2140317447749652479)
XLA Ops:
  0.0 0.7 iota_compare_fusion.2
  0.7 0.8 %multiply_reduce_fusion = f32[64,4]{0,1:T(4,128)S(1)} fusion(f32[64,16]{0,1:T(8,128)} %param.15, s32[64]{0:T(128)} %param.18, s32[64,4]{0,1:T(4,128)} %param.19, pred[64,16]{0,1:T(8,128)(4,1)S(1)} %iota_compare_fusion.2), kind=kLoop, calls=%fused_computation.8 | loop fusion | flops 40704 | bytes 7424 | tf_op jit(solution)/shard_map/reduce_sum | solution.py:39
  1.4 0.7 add_minimum_fusion
  2.1 0.7 add_bitcast_fusion
  2.8 0.1 eq.35
  2.9 0.2 eq.36
  3.1 0.0 copy-start.1
  3.1 0.0 copy-start
  3.1 0.0 copy-start.2
  3.1 0.9 %convert_reduce_fusion = s32[64]{0:T(128)S(1)} fusion(s32[64]{0:T(128)} %bitcast.32), kind=kLoop, calls=%fused_computation.6 | loop fusion | flops 20416 | bytes 512 | tf_op jit(solution)/shard_map/reduce_sum | solution.py:27
  4.0 0.7 fusion.15
  4.7 0.1 broadcast_in_dim.24
  4.8 0.1 broadcast_in_dim.25
  4.9 0.1 eq.38
  5.0 0.6 compare_select_fusion.key_ref
  5.6 0.7 convert.17
  6.3 0.1 copy.42
  6.4 0.1 stack.18
  6.5 0.1 copy.43
  6.6 0.1 stack.19
  6.7 0.1 copy.44
  6.8 0.1 stack.20
  6.9 0.1 copy.45
  7.0 0.1 stack.21
  7.1 0.1 copy.46
  7.2 0.1 stack.22
  7.3 0.2 copy.47
  7.5 0.8 %pad.8.acts_ref = bf16[1024,128]{1,0:T(8,128)(2,1)} pad(bf16[1024,5]{1,0:T(8,128)(2,1)S(1)} %copy.47, bf16[]{:T(256)} %constant.41.clone.1), padding=0_0x0_123 | pad | bytes 272386 | tf_op jit(solution)/shard_map/jit(_pad)/pad | solution.py:410
  8.3 1.2 %fusion.17.spot_ref = s32[1,64]{1,0:T(1,128)} fusion(s32[64]{0:T(128)S(1)} %convert_reduce_fusion, s32[64,1]{0,1:T(1,128)} %param.20, s32[]{:T(128)S(6)} %axis_index.15), kind=kLoop, calls=%fused_computation.36 | loop fusion | flops 1344 | bytes 772 | tf_op jit(solution)/shard_map/add | solution.py:400
  9.5 1.4 %fusion.4.small_ref = bf16[32,512]{1,0:T(8,128)(2,1)} fusion(bf16[1,512]{1,0:T(2,128)(2,1)} %param.27, bf16[1,512]{1,0:T(2,128)(2,1)} %param.26, bf16[18,512]{1,0:T(8,128)(2,1)} %bitcast.31), kind=kLoop, calls=%fused_computation.5 | loop fusion | flops 163840 | bytes 53248 | tf_op jit(solution)/shard_map/concatenate | solution.py:394
  10.8 61.1 %shard_map.136 = f32[8,64]{1,0:T(8,128)} custom-call(bf16[1024,1024]{1,0:T(8,128)(2,1)} %bitcast.26, s32[8,1024]{1,0:T(8,128)} %compare_select_fusion.key_ref, bf16[1024,128]{1,0:T(8,128)(2,1)} %pad.8.acts_ref, s32[1,64]{1,0:T(1,128)} %fusion.17.spot_ref, bf16[128,512]{1,0:T(8,128)(2,1)} %bitcast.27, bf16[64,512]{1,0:T(8,128)(2,1)} %bitcast.28, ...), custom_call_target="tpu_custom_call" | custom-call | tf_op jit(solution)/shard_map/pallas_call | solution.py:417
  71.9 0.0 copy-done.1
  72.0 0.0 copy-done
  72.0 0.0 copy-done.2
  72.0 1.3 %fusion.10 = f32[64,4]{0,1:T(4,128)} fusion(f32[64,4]{0,1:T(4,128)S(1)} %multiply_reduce_fusion, f32[8,64]{1,0:T(8,128)} %shard_map.136, s32[64,4]{0,1:T(4,128)S(1)} %copy-done, f32[64]{0:T(128)S(1)} %convert_power_fusion, s32[64]{0:T(128)S(1)} %copy-done.2, s32[64]{0:T(128)S(1)} %copy-done.1), kind=kLoop, calls=%fused_computation.25 | loop fusion | flops 1792 | bytes 5888 | tf_op jit(solution)/shard_map/abs | solution.py:456
  (4 shorter events, 0.1 us)
Async XLA Ops:
  3.1 68.8 %copy-start.1 = (s32[64]{0:T(128)S(1)}, s32[64]{0:T(128)}, u32[]{:S(2)}) copy-start(s32[64]{0:T(128)} %param.18) | copy-start | bytes 772
  3.1 68.9 %copy-start = (s32[64,4]{0,1:T(4,128)S(1)}, s32[64,4]{0,1:T(4,128)}, u32[]{:S(2)}) copy-start(s32[64,4]{0,1:T(4,128)} %param.19) | copy-start | bytes 3076
  3.1 68.9 %copy-start.2 = (s32[64]{0:T(128)S(1)}, s32[64]{0:T(128)}, u32[]{:S(2)}) copy-start(s32[64]{0:T(128)} %param.17) | copy-start | bytes 772
